TPU v7x, 32 devices: a whole 2x2x4 slice. The times are simulated.
32 devices in a mesh: col: 8 (over z, y), row: 4 (over x, core).
Axes of the slice: x: 2, y: 2, z: 4, core: 2. Of those that a mesh axis runs over, the one named last changes fastest.
Arguments:
- right_side: float32 [8192, 256], P(('row', 'col')), may hold values from -6 to 6
- prior_solution: bfloat16 [16384, 256], P('col'), may hold values from -6 to 6
- factor_codes: bfloat16 [8192, 16384], P('row', 'col'), may hold values from -0.046875 to 0.046875
- block_scale: float32 [4, 64], P('row', 'col'), may hold values from 0.3 to 3
- diag_inverse: bfloat16 [4, 2048, 2048], P('row', 'col'), may hold values from -0.125 to 0.125
- inner_factor: bfloat16 [4, 4, 2048, 2048], P('row', None, 'col'), may hold values from -0.125 to 0.125
Outputs:
- solved: float32 [8192, 256], P(('row', 'col'))
All inputs are finite; a program needn't handle non-finite values.
Results may differ from a plain program's by a relative error of at most 0.0095.
Values may be sent and summed in bfloat16 or wider, within the bound.
No kernel may reach another device: no remote copies, remote signals or barrier semaphores. Data moves between devices by JAX's collectives and lax.ppermute only.
A program may use at most 64 MiB of HBM per device.

v0:
```python
import jax
import jax.numpy as jnp
from jax import lax
from jax.sharding import PartitionSpec as P


def from_root(value, axis, source):
    kept = jnp.where(lax.axis_index(axis) == source, value, 0).astype(value.dtype)
    return lax.psum(kept, axis)


def local(right_side, prior_solution, factor_codes, block_scale, diag_inverse, inner_factor):
    rows_each = right_side.shape[0]
    panel_rows = factor_codes.shape[0]
    blocks_here = block_scale.shape[1]
    block_cols = factor_codes.shape[1] // blocks_here
    columns_out = right_side.shape[1]
    summed = jnp.zeros((panel_rows, columns_out), jnp.float32)
    for column_block in range(blocks_here):
        coded = lax.dynamic_slice(
            factor_codes, (0, column_block * block_cols), (panel_rows, block_cols)
        )
        earlier = prior_solution[column_block * block_cols : (column_block + 1) * block_cols]
        summed = summed + block_scale[0, column_block] * jnp.dot(
            coded, earlier, preferred_element_type=jnp.float32
        )
    prior_rows = lax.psum_scatter(summed, "col", scatter_dimension=0, tiled=True)
    rhs = right_side - prior_rows
    row_place = lax.axis_index("row")
    solved = jnp.zeros((rows_each, columns_out), jnp.float32)
    inverse_rows = diag_inverse[0]
    panel_count = lax.axis_size("row")
    for section in range(panel_count):
        rounded = rhs.astype(jnp.bfloat16)
        current = jnp.dot(
            inverse_rows,
            lax.all_gather(rounded, "col", axis=0, tiled=True),
            preferred_element_type=jnp.float32,
        )
        solved = jnp.where(row_place == section, current, solved)
        if section + 1 < panel_count:
            sending = current.astype(jnp.bfloat16)
            coupling = inner_factor[0, section]
            whole_panel = lax.all_gather(sending, "col", axis=0, tiled=True)
            copied = from_root(whole_panel, "row", section)
            update = jnp.dot(coupling, copied, preferred_element_type=jnp.float32)
            rhs = rhs - jnp.where(row_place > section, update, 0.0)
    return solved


def solution(mesh):
    return jax.shard_map(
        local,
        mesh=mesh,
        in_specs=(
            P(("row", "col"), None),
            P("col", None),
            P("row", "col"),
            P("row", "col"),
            P("row", "col", None),
            P("row", None, "col", None),
        ),
        out_specs=P(("row", "col"), None),
        check_vma=False,
    )
```

profile of v0, /device:TPU:0, one launch (start us, length us, event | category | flops | bytes accessed | tf_op | source)
XLA Modules:
  0.0 509.4 jit_solution(15707440207164434849)
XLA Ops:
  6.5 0.0 copy-start
  6.5 0.0 reduce-scatter.2.cloned.1.call-start
  6.5 1.6 fusion.45
  8.2 2.5 convolution_multiply_fusion.7
  10.7 2.5 fusion.6
  13.3 0.0 copy-done.1
  13.3 0.0 copy-start.2
  13.3 2.0 fusion.5
  15.3 0.0 copy-done.2
  15.3 1.1 fusion.4
  16.4 1.1 fusion.3
  17.5 1.1 fusion.2
  18.6 1.0 fusion.1
  19.6 2.4 fusion
  22.0 0.0 reduce-scatter.2.cloned.1.call-update
  22.0 0.0 all-gather.8.cloned.1.call-start
  22.1 71.2 %reduce-scatter.2.cloned.1.call-done = f32[256,256]{1,0:T(8,128)} async-done(((f32[2048,256]{1,0:T(8,128)}), f32[256,256]{1,0:T(8,128)}) %reduce-scatter.2.cloned.1.call-update) | async-done | bytes 262160 | tf_op jit(solution)/shard_map/reduce_scatter | solution.py:27
  93.2 1.6 fusion.44
  94.9 0.0 all-gather.8.cloned.1.call-update
  94.9 0.0 all-gather.10.cloned.1.call-start
  95.0 39.7 %all-gather.8.cloned.1.call-done = bf16[2048,256]{1,0:T(8,128)(2,1)} async-done(((bf16[256,256]{1,0:T(8,128)(2,1)}), bf16[2048,256]{1,0:T(8,128)(2,1)}) %all-gather.8.cloned.1.call-update) | async-done | bytes 1048592 | tf_op jit(solution)/shard_map/all_gather | solution.py:37
  134.7 0.0 copy-done
  134.7 1.7 fusion.23
  136.4 0.7 convert_bitcast_fusion.2
  137.1 0.0 all-gather.10.cloned.1.call-update
  137.1 0.0 all-reduce.4.cloned.1.call-start
  137.2 38.2 %all-gather.10.cloned.1.call-done = bf16[2048,256]{0,1:T(8,128)(2,1)} async-done(((bf16[256,256]{0,1:T(8,128)(2,1)}), bf16[2048,256]{0,1:T(8,128)(2,1)}) %all-gather.10.cloned.1.call-update) | async-done | bytes 1048592 | tf_op jit(solution)/shard_map/all_gather | solution.py:44
  175.4 2.3 broadcast_select_fusion.2
  177.7 0.0 all-reduce.4.cloned.1.call-update
  177.7 0.0 all-gather.12.cloned.1.call-start
  177.7 35.2 %all-reduce.4.cloned.1.call-done = bf16[2048,256]{0,1:T(8,128)(2,1)} async-done(((bf16[2048,256]{0,1:T(8,128)(2,1)}), bf16[2048,256]{0,1:T(8,128)(2,1)}) %all-reduce.4.cloned.1.call-update) | async-done | bytes 1048592 | tf_op jit(solution)/shard_map/psum | solution.py:9
  212.9 2.7 fusion.46
  215.6 0.0 all-gather.12.cloned.1.call-update
  215.6 0.0 all-gather.14.cloned.1.call-start
  215.7 40.9 %all-gather.12.cloned.1.call-done = bf16[2048,256]{1,0:T(8,128)(2,1)} async-done(((bf16[256,256]{1,0:T(8,128)(2,1)}), bf16[2048,256]{1,0:T(8,128)(2,1)}) %all-gather.12.cloned.1.call-update) | async-done | bytes 1048592 | tf_op jit(solution)/shard_map/all_gather | solution.py:37
  256.5 1.7 fusion.21
  258.2 0.7 convert_bitcast_fusion.1
  258.9 0.0 all-gather.14.cloned.1.call-update
  258.9 0.0 all-reduce.6.cloned.1.call-start
  259.0 38.2 %all-gather.14.cloned.1.call-done = bf16[2048,256]{0,1:T(8,128)(2,1)} async-done(((bf16[256,256]{0,1:T(8,128)(2,1)}), bf16[2048,256]{0,1:T(8,128)(2,1)}) %all-gather.14.cloned.1.call-update) | async-done | bytes 1048592 | tf_op jit(solution)/shard_map/all_gather | solution.py:44
  297.2 1.1 broadcast_select_fusion.1
  298.3 0.0 all-reduce.6.cloned.1.call-update
  298.3 0.0 all-gather.16.cloned.1.call-start
  298.3 36.5 %all-reduce.6.cloned.1.call-done = bf16[2048,256]{0,1:T(8,128)(2,1)} async-done(((bf16[2048,256]{0,1:T(8,128)(2,1)}), bf16[2048,256]{0,1:T(8,128)(2,1)}) %all-reduce.6.cloned.1.call-update) | async-done | bytes 1048592 | tf_op jit(solution)/shard_map/psum | solution.py:9
  334.9 2.7 fusion.47
  337.6 0.0 all-gather.16.cloned.1.call-update
  337.6 0.0 all-gather.18.cloned.1.call-start
  337.6 40.9 %all-gather.16.cloned.1.call-done = bf16[2048,256]{1,0:T(8,128)(2,1)} async-done(((bf16[256,256]{1,0:T(8,128)(2,1)}), bf16[2048,256]{1,0:T(8,128)(2,1)}) %all-gather.16.cloned.1.call-update) | async-done | bytes 1048592 | tf_op jit(solution)/shard_map/all_gather | solution.py:37
  378.5 1.7 fusion.19
  380.2 0.7 convert_bitcast_fusion
  380.9 0.0 all-gather.18.cloned.1.call-update
  380.9 0.0 all-reduce.8.cloned.1.call-start
  381.0 38.2 %all-gather.18.cloned.1.call-done = bf16[2048,256]{0,1:T(8,128)(2,1)} async-done(((bf16[256,256]{0,1:T(8,128)(2,1)}), bf16[2048,256]{0,1:T(8,128)(2,1)}) %all-gather.18.cloned.1.call-update) | async-done | bytes 1048592 | tf_op jit(solution)/shard_map/all_gather | solution.py:44
  419.2 1.1 broadcast_select_fusion
  420.2 0.0 all-reduce.8.cloned.1.call-update
  420.2 0.0 all-gather.20.cloned.1.call-start
  420.3 36.6 %all-reduce.8.cloned.1.call-done = bf16[2048,256]{0,1:T(8,128)(2,1)} async-done(((bf16[2048,256]{0,1:T(8,128)(2,1)}), bf16[2048,256]{0,1:T(8,128)(2,1)}) %all-reduce.8.cloned.1.call-update) | async-done | bytes 1048592 | tf_op jit(solution)/shard_map/psum | solution.py:9
  456.9 2.7 fusion.14
  459.6 0.0 all-gather.20.cloned.1.call-update
  459.6 0.1 copy.9
  459.8 0.1 copy.10
  459.9 0.1 copy.11
  460.0 40.5 %all-gather.20.cloned.1.call-done = bf16[2048,256]{1,0:T(8,128)(2,1)} async-done(((bf16[256,256]{1,0:T(8,128)(2,1)}), bf16[2048,256]{1,0:T(8,128)(2,1)}) %all-gather.20.cloned.1.call-update) | async-done | bytes 1048592 | tf_op jit(solution)/shard_map/all_gather | solution.py:37
  500.5 2.4 fusion.7
  (3 shorter events, 0.0 us)
Async XLA Ops:
  6.5 128.2 %copy-start = (bf16[1,256,2048]{2,1,0:T(8,128)(2,1)S(1)}, bf16[1,256,2048]{2,1,0:T(8,128)(2,1)}, u32[]{:S(2)}) copy-start(bf16[1,256,2048]{2,1,0:T(8,128)(2,1)} %param.10) | copy-start | bytes 3145732
  6.5 86.7 %reduce-scatter.2.cloned.1.call-start = ((), (), s32[]{:S(2)}) async-start(), calls=%async_computation.1 | async-start | bytes 2359296 | tf_op jit(solution)/shard_map/reduce_scatter | solution.py:27
  8.2 5.1 copy-start.1
  13.3 2.0 copy-start.2
  22.0 71.2 %copy-start.3 = (f32[256,256]{1,0:T(8,128)S(1)}, f32[256,256]{1,0:T(8,128)}, u32[]{:S(2)}) copy-start(f32[256,256]{1,0:T(8,128)} %param.6) | copy-start | bytes 786436
  22.0 112.7 %all-gather.8.cloned.1.call-start = ((), (), s32[]{:S(2)}) async-start(), calls=%async_computation.2 | async-start | bytes 1179648 | tf_op jit(solution)/shard_map/all_gather | solution.py:37
  94.9 80.5 %all-gather.10.cloned.1.call-start = ((), (), s32[]{:S(2)}) async-start(), calls=%async_computation.3 | async-start | bytes 1179648 | tf_op jit(solution)/shard_map/all_gather | solution.py:44
  137.1 75.8 %all-reduce.4.cloned.1.call-start = ((), (), s32[]{:S(2)}) async-start(), calls=%async_computation.4 | async-start | bytes 2097152 | tf_op jit(solution)/shard_map/psum | solution.py:9
  177.7 78.9 %all-gather.12.cloned.1.call-start = ((), (), s32[]{:S(2)}) async-start(), calls=%async_computation.5 | async-start | bytes 1179648 | tf_op jit(solution)/shard_map/all_gather | solution.py:37
  215.6 81.6 %all-gather.14.cloned.1.call-start = ((), (), s32[]{:S(2)}) async-start(), calls=%async_computation.6 | async-start | bytes 1179648 | tf_op jit(solution)/shard_map/all_gather | solution.py:44
  258.9 75.9 %all-reduce.6.cloned.1.call-start = ((), (), s32[]{:S(2)}) async-start(), calls=%async_computation.7 | async-start | bytes 2097152 | tf_op jit(solution)/shard_map/psum | solution.py:9
  298.3 80.2 %all-gather.16.cloned.1.call-start = ((), (), s32[]{:S(2)}) async-start(), calls=%async_computation.8 | async-start | bytes 1179648 | tf_op jit(solution)/shard_map/all_gather | solution.py:37
  337.6 81.6 %all-gather.18.cloned.1.call-start = ((), (), s32[]{:S(2)}) async-start(), calls=%async_computation.9 | async-start | bytes 1179648 | tf_op jit(solution)/shard_map/all_gather | solution.py:44
  380.9 76.0 %all-reduce.8.cloned.1.call-start = ((), (), s32[]{:S(2)}) async-start(), calls=%async_computation.10 | async-start | bytes 2097152 | tf_op jit(solution)/shard_map/psum | solution.py:9
  420.2 80.3 %all-gather.20.cloned.1.call-start = ((), (), s32[]{:S(2)}) async-start(), calls=%async_computation.11 | async-start | bytes 1179648 | tf_op jit(solution)/shard_map/all_gather | solution.py:37
Sparse Core Ops, SparseCore 0:
  22.2 71.0 reduce-scatter.1
  95.4 39.2 all-gather.7
  137.2 38.0 all-gather.9
  177.8 35.0 all-reduce.3
  215.8 40.7 all-gather.11
  259.1 38.0 all-gather.13
  299.6 35.2 all-reduce.5
  337.7 40.7 all-gather.15
  381.0 38.0 all-gather.17
  421.4 35.4 all-reduce.7
  459.7 40.7 all-gather.19
where the time goes:
time: 510 us; the launch traced here: 509 us
  waiting for transfers between devices  456 us (89%)
  matrix products  29.3 us (6%)
  between operations  13.4 us (3%)
  other arithmetic  8.06 us (2%)
    all_gather x4, waiting for transfers between devices, local(): lax.all_gather(rounded, 'col', axis=0, tiled=True)  162 us
    all_gather x3, waiting for transfers between devices, local(): whole_panel = lax.all_gather(sending, 'col', axis=0, tiled=True)  115 us
    psum x3, waiting for transfers between devices, from_root(): return lax.psum(kept, axis)  108 us
    reduce_scatter x1, waiting for transfers between devices, local(): lax.psum_scatter(summed, 'col', scatter_dimension=0, tiled=True)  71.2 us
    dot_general x8, matrix products, local(): jnp.dot(coded, earlier, preferred_element_type=jnp.float32)  13.7 us
  transfers between devices with their start and end apart: 11, of which 11 were waited for; matrix products, arithmetic and copies ran while one was open for 0% of the time, Pallas kernels for 0%

commit v1 on v0

v1 whole, which is shorter than its diff:
```python
import jax
import jax.numpy as jnp
from jax import lax
from jax.sharding import Mesh, PartitionSpec as P

AXES = ("cz", "cy", "rx", "rc")


def solution(mesh):
    cols, rows = mesh.shape["col"], mesh.shape["row"]
    sizes = (cols // 2, 2, rows // 2, 2)
    grid = Mesh(mesh.devices.reshape(sizes), AXES)
    count_z, _, count_x, _ = sizes
    bf16 = jnp.bfloat16

    def place(z, y, x, c):
        return ((z * 2 + y) * sizes[2] + x) * 2 + c

    def send(value, target, only=None):
        pairs = []
        for z in range(sizes[0]):
            for y in range(2):
                for x in range(sizes[2]):
                    for c in range(2):
                        if only is None or only(z, y, x, c):
                            pairs.append((place(z, y, x, c), place(*target(z, y, x, c))))
        return lax.ppermute(value, AXES, pairs)

    def over_y(z, y, x, c):
        return z, 1 - y, x, c

    def over_core(z, y, x, c):
        return z, y, x, 1 - c

    def odd_only(z, y, x, c):
        return c == 1

    def later_only(z, y, x, c):
        return x > 0

    def local(right_side, prior_solution, factor_codes, block_scale, diag_inverse, inner_factor):
        each, width = right_side.shape
        part = width // 4
        zed, why = lax.axis_index("cz"), lax.axis_index("cy")
        ex, core = lax.axis_index("rx"), lax.axis_index("rc")
        chunk = 2 * each
        panel = factor_codes.shape[0]

        def gather(piece):
            if count_z > 4:
                return jnp.moveaxis(lax.all_gather(piece, "cz", axis=0), 0, 1).reshape(part, panel)
            whole = jnp.zeros((part, panel), piece.dtype)
            got = [(zed, piece)]
            for step in range(1, count_z):
                moved = lax.ppermute(
                    piece, "cz", [(i, (i + step) % count_z) for i in range(count_z)]
                )
                got.append((lax.rem(zed + count_z - step, count_z), moved))
            for source, value in got:
                whole = lax.dynamic_update_slice(whole, value, (0, source * chunk))
            return whole

        def both_rows(inverse):
            beside = send(inverse, over_y)
            return inverse, beside

        def apply(pieces, vector):
            mine, beside = [
                lax.dot_general(
                    vector, piece, (((1,), (1,)), ((), ())), preferred_element_type=jnp.float32
                )
                for piece in pieces
            ]
            first = jnp.where(why == 0, mine, beside)
            second = jnp.where(why == 0, beside, mine)
            return jnp.concatenate([first, second], axis=1)

        def pick(even, odd):
            return jnp.where(core == 0, even, odd)

        inverse = diag_inverse[0]
        inverse_y = send(inverse, over_y)
        inverse_c = send(inverse, over_core)
        inverse_yc = send(inverse_y, over_core)
        inv_even = (pick(inverse, inverse_c), pick(inverse_y, inverse_yc))
        inv_odd = (pick(inverse_c, inverse), pick(inverse_yc, inverse_y))
        pair = lax.dynamic_index_in_dim(inner_factor[0], 2 * ex, 0, keepdims=False)
        pair_y = send(pair, over_y, odd_only)
        pair_c = send(pair, over_core, odd_only)
        pair_yc = send(pair_y, over_core, odd_only)
        link = (pick(pair_c, pair), pick(pair_yc, pair_y))
        before = 2 * (count_x - 1)
        past = inner_factor[0, :before]
        past_y = send(past, over_y, later_only)
        past_c = send(past, over_core, later_only)
        past_yc = send(past_y, over_core, later_only)
        past_even = (pick(past, past_c), pick(past_y, past_yc))
        past_odd = (pick(past_c, past), pick(past_yc, past_y))

        blocks = block_scale.shape[1]
        block_cols = prior_solution.shape[0] // blocks
        scaled = (
            prior_solution.astype(jnp.float32).reshape(blocks, block_cols, width)
            * block_scale[0][:, None, None]
        ).reshape(-1, width).astype(bf16)
        product = lax.dot_general(
            scaled, factor_codes, (((0,), (1,)), ((), ())), preferred_element_type=jnp.float32
        )
        spot = (zed * 2 + why) * each
        mine = lax.dynamic_slice(product, (0, spot), (width, each))
        partial = lax.dynamic_update_slice(-product, right_side.T - mine, (0, spot))
        parts = partial.astype(bf16).reshape(2, 2, part, count_z, chunk).transpose(3, 0, 1, 2, 4)
        parts = parts.reshape(count_z * 4, part, chunk)
        came = lax.all_to_all(parts, ("cz", "cy", "rc"), 0, 0)
        came = came.reshape(count_z * 2, 2, part, chunk).astype(jnp.float32).sum(0)
        rhs_even, rhs_odd = came[0], came[1]

        for turn in range(count_x):
            even = apply(inv_even, gather(rhs_even.astype(bf16)))
            even_all = gather(even.astype(bf16))
            current = rhs_odd - apply(link, even_all)
            odd = apply(inv_odd, gather(current.astype(bf16)))
            for later in range(turn + 1, count_x):

                def to_later(z, y, x, c):
                    return z, y, later, c

                def from_turn(z, y, x, c):
                    return x == turn

                seen_even = send(even_all, to_later, from_turn)
                seen_odd = gather(send(odd.astype(bf16), to_later, from_turn))
                for index, seen in ((2 * turn, seen_even), (2 * turn + 1, seen_odd)):
                    rhs_even = rhs_even - apply([p[index] for p in past_even], seen)
                    rhs_odd = rhs_odd - apply([p[index] for p in past_odd], seen)

        out = jnp.stack([even, odd]).reshape(2, part, 2, each).transpose(2, 0, 1, 3)
        out = lax.all_to_all(out.reshape(4, part, each), ("cy", "rc"), 0, 0)
        return out.reshape(width, each).T

    return jax.shard_map(
        local,
        mesh=grid,
        in_specs=(
            P(("rx", "rc", "cz", "cy"), None),
            P(("cz", "cy"), None),
            P(("rx", "rc"), ("cz", "cy")),
            P(("rx", "rc"), ("cz", "cy")),
            P(("rx", "rc"), ("cz", "cy"), None),
            P(("rx", "rc"), None, ("cz", "cy"), None),
        ),
        out_specs=P(("rx", "rc", "cz", "cy"), None),
        check_vma=False,
    )
```

time: 510 us -> 184 us (0.36)
  waiting for transfers between devices: 456 us -> 71.2 us
  starting transfers between devices: 0.42 us -> 66.7 us
  between operations: 13.4 us -> 0.58 us
  blocking collectives: 0 us -> 8.39 us
  local copies, waits for them, and re-layouts: 2.03 us -> 9.71 us
  matrix products: 29.3 us -> 23.6 us
  other arithmetic: 8.06 us -> 2.51 us
    all_gather x7 -> x0, waiting for transfers between devices: 277 us -> none  [the longest x4 162 us: local(): lax.all_gather(rounded, 'col', axis=0, tiled=True)]
    psum x3 -> x0, waiting for transfers between devices: 108 us -> none  [from_root(): return lax.psum(kept, axis)]
    ppermute x0 -> x32, waiting for transfers between devices: none -> 71.2 us  [the longest x21 37.9 us: gather(): lax.ppermute(piece, 'cz', [(i, (i + step) % count_z) for i in range(count...]
    reduce_scatter x1 -> x0, waiting for transfers between devices: 71.2 us -> none  [local(): lax.psum_scatter(summed, 'col', scatter_dimension=0, tiled=True)]
    ppermute x0 -> x32, starting transfers between devices: none -> 59.3 us  [the longest x21 29.7 us: gather(): lax.ppermute(piece, 'cz', [(i, (i + step) % count_z) for i in range(count...]
    all_to_all x0 -> x1, blocking collectives: none -> 8.39 us  [local(): out = lax.all_to_all(out.reshape(4, part, each), ('cy', 'rc'), 0, 0)]
    all_to_all x0 -> x1, starting transfers between devices: none -> 7.42 us  [local(): came = lax.all_to_all(parts, ('cz', 'cy', 'rc'), 0, 0)]
    dot_general x15 -> x21, matrix products: 29.3 us -> 23.6 us  [the longest x20 17.1 us: apply(): lax.dot_general(vector, piece, (((1,), (1,)), ((), ())), preferred_elemen...]
  transfers between devices with their start and end apart: 11 -> 33, of which waited for: 11 -> 20; matrix products, arithmetic and copies ran while one was open for 0% -> 9% of each run, Pallas kernels for 0% -> 0%
where the time goes in v1:
time: 184 us; the launch traced here: 183 us
  waiting for transfers between devices  71.2 us (39%)
  starting transfers between devices  66.7 us (36%)
  matrix products  23.6 us (13%)
  local copies, waits for them, and re-layouts  9.71 us (5%)
  blocking collectives  8.39 us (5%)
  other arithmetic  2.51 us (1%)
    ppermute x21, waiting for transfers between devices, gather(): lax.ppermute(piece, 'cz', [(i, (i + step) % count_z) for i in range(count...  37.9 us
    ppermute x11, waiting for transfers between devices, send(): return lax.ppermute(value, AXES, pairs)  33.3 us
    ppermute x21, starting transfers between devices, gather(): lax.ppermute(piece, 'cz', [(i, (i + step) % count_z) for i in range(count...  29.7 us
    ppermute x11, starting transfers between devices, send(): return lax.ppermute(value, AXES, pairs)  29.6 us
    dot_general x20, matrix products, apply(): lax.dot_general(vector, piece, (((1,), (1,)), ((), ())), preferred_elemen...  17.1 us
    all_to_all x1, blocking collectives, local(): out = lax.all_to_all(out.reshape(4, part, each), ('cy', 'rc'), 0, 0)  8.39 us
    all_to_all x1, starting transfers between devices, local(): came = lax.all_to_all(parts, ('cz', 'cy', 'rc'), 0, 0)  7.42 us
    dot_general x1, matrix products, local(): lax.dot_general(scaled, factor_codes, (((0,), (1,)), ((), ())), preferred...  6.47 us
  transfers between devices with their start and end apart: 33, of which 20 were waited for; matrix products, arithmetic and copies ran while one was open for 9% of the time, Pallas kernels for 0%

profile of v1, /device:TPU:0, one launch (start us, length us, event | category | flops | bytes accessed | tf_op | source)
XLA Modules:
  0.0 182.7 jit_solution(11758541827056040749)
XLA Ops:
  0.0 0.7 copy-done
  0.7 1.1 copy.8
  1.8 6.5 %fusion.40 = (bf16[256,2048]{1,0:T(8,128)(2,1)S(1)}, f32[256,2048]{1,0:T(8,128)S(1)}) fusion(bf16[2048,2048]{1,0:T(8,128)(2,1)} %param.8, bf16[2048,256]{1,0:T(8,128)(2,1)} %param.7, f32[2048]{0:T(1024)S(1)} %bitcast.117), kind=kOutput, calls=%fused_computation.117 | convolution fusion | flops 2150105088 | bytes 12591104 | tf_op jit(solution)/shard_map/dot_general | solution.py:106
  8.3 0.8 reshape.26
  9.1 1.2 copy.9
  10.4 7.4 %all-to-all-start = ((bf16[16,64,512]{2,1,0:T(8,128)(2,1)}), bf16[16,64,512]{2,1,0:T(8,128)(2,1)S(1)}, u32[]{:S(2)}, u32[]{:S(2)}) async-start(bf16[16,64,512]{2,1,0:T(8,128)(2,1)} %bitcast.3), calls=%async_computation | async-start | bytes 2097152 | tf_op jit(solution)/shard_map/all_to_all | solution.py:114
  17.8 1.9 %collective-permute-start.4 = (bf16[256,2048]{1,0:T(8,128)(2,1)}, bf16[256,2048]{1,0:T(8,128)(2,1)S(1)}, u32[]{:S(2)}, u32[]{:S(2)}) collective-permute-start(bf16[256,2048]{1,0:T(8,128)(2,1)} %bitcast.6), channel_id=1, source_target_pairs={{0,4},{1,5},{2,6},{3,7},{4,0},{5,1},{6,2},{7,3},{8,12},{9,13},{10,... | collective-permute-start | bytes 3145736 | tf_op jit(solution)/shard_map/ppermute | solution.py:27
  19.7 1.3 dynamic-slice_bitcast_fusion
  21.1 1.6 collective-permute-start.14
  22.7 32.5 %collective-permute-done.4 = bf16[256,2048]{1,0:T(8,128)(2,1)S(1)} collective-permute-done((bf16[256,2048]{1,0:T(8,128)(2,1)}, bf16[256,2048]{1,0:T(8,128)(2,1)S(1)}, u32[]{:S(2)}, u32[]{:S(2)}) %collective-permute-start.4) | collective-permute-done | bytes 1048608 | tf_op jit(solution)/shard_map/ppermute | solution.py:27
  55.4 1.5 collective-permute-start
  56.9 3.2 %slice_bitcast_fusion = bf16[2,256,2048]{2,1,0:T(8,128)(2,1)} fusion(bf16[1,4,256,2048]{3,2,1,0:T(8,128)(2,1)} %param.11), kind=kLoop, calls=%fused_computation.1 | loop fusion | bytes 4194304 | tf_op jit(solution)/shard_map/squeeze | solution.py:93
  60.1 2.0 %collective-permute-start.11 = (bf16[2,256,2048]{2,1,0:T(8,128)(2,1)}, bf16[2,256,2048]{2,1,0:T(8,128)(2,1)}, u32[]{:S(2)}, u32[]{:S(2)}) collective-permute-start(bf16[2,256,2048]{2,1,0:T(8,128)(2,1)} %slice_bitcast_fusion), channel_id=1, source_target_pairs={{2,6},{3,7},{6,2},{7,3},{10,14},{11,15},{14,10},{15,11},{18,22},{1... | collective-permute-start | bytes 6291464 | tf_op jit(solution)/shard_map/ppermute | solution.py:27
  62.1 2.4 %collective-permute-start.1 = (bf16[64,512]{1,0:T(8,128)(2,1)S(1)}, bf16[64,512]{1,0:T(8,128)(2,1)S(1)}, u32[]{:S(2)}, u32[]{:S(2)}) collective-permute-start(bf16[64,512]{1,0:T(8,128)(2,1)S(1)} %get-tuple-element.14), channel_id=1, source_target_pairs={{0,16},{8,24},{16,0},{24,8},{1,17},{9,25},{17,1},{25,9},{2,18},{10... | collective-permute-start | bytes 196616 | tf_op jit(solution)/shard_map/ppermute | solution.py:55
  64.4 4.2 %collective-permute-done.1 = bf16[64,512]{1,0:T(8,128)(2,1)S(1)} collective-permute-done((bf16[64,512]{1,0:T(8,128)(2,1)S(1)}, bf16[64,512]{1,0:T(8,128)(2,1)S(1)}, u32[]{:S(2)}, u32[]{:S(2)}) %collective-permute-start.1) | collective-permute-done | bytes 65568 | tf_op jit(solution)/shard_map/ppermute | solution.py:55
  68.6 2.4 %collective-permute-start.2 = (bf16[64,512]{1,0:T(8,128)(2,1)S(1)}, bf16[64,512]{1,0:T(8,128)(2,1)S(1)}, u32[]{:S(2)}, u32[]{:S(2)}) collective-permute-start(bf16[64,512]{1,0:T(8,128)(2,1)S(1)} %get-tuple-element.14), channel_id=1, source_target_pairs={{0,24},{8,0},{16,8},{24,16},{1,25},{9,1},{17,9},{25,17},{2,26},{10... | collective-permute-start | bytes 196616 | tf_op jit(solution)/shard_map/ppermute | solution.py:55
  71.0 1.3 collective-permute-start.13
  72.3 0.6 collective-permute-done.2
  72.9 1.3 collective-permute-start.15
  74.2 1.7 fusion.11
  75.9 0.5 select_convert_fusion.3
  76.6 0.8 collective-permute-start.10
  77.4 5.5 %collective-permute-done.6 = bf16[64,512]{1,0:T(8,128)(2,1)S(1)} collective-permute-done((bf16[64,512]{1,0:T(8,128)(2,1)S(1)}, bf16[64,512]{1,0:T(8,128)(2,1)S(1)}, u32[]{:S(2)}, u32[]{:S(2)}) %collective-permute-start.6) | collective-permute-done | bytes 65568 | tf_op jit(solution)/shard_map/ppermute | solution.py:55
  83.1 6.1 %collective-permute-done.7 = bf16[64,512]{1,0:T(8,128)(2,1)S(1)} collective-permute-done((bf16[64,512]{1,0:T(8,128)(2,1)S(1)}, bf16[64,512]{1,0:T(8,128)(2,1)S(1)}, u32[]{:S(2)}, u32[]{:S(2)}) %collective-permute-start.7) | collective-permute-done | bytes 65568 | tf_op jit(solution)/shard_map/ppermute | solution.py:55
  89.2 2.1 %collective-permute-start.8 = (bf16[64,512]{1,0:T(8,128)(2,1)S(1)}, bf16[64,512]{1,0:T(8,128)(2,1)S(1)}, u32[]{:S(2)}, u32[]{:S(2)}) collective-permute-start(bf16[64,512]{1,0:T(8,128)(2,1)S(1)} %get-tuple-element.37), channel_id=1, source_target_pairs={{0,24},{8,0},{16,8},{24,16},{1,25},{9,1},{17,9},{25,17},{2,26},{10... | collective-permute-start | bytes 196616 | tf_op jit(solution)/shard_map/ppermute | solution.py:55
  91.4 2.2 %collective-permute-done.8 = bf16[64,512]{1,0:T(8,128)(2,1)S(1)} collective-permute-done((bf16[64,512]{1,0:T(8,128)(2,1)S(1)}, bf16[64,512]{1,0:T(8,128)(2,1)S(1)}, u32[]{:S(2)}, u32[]{:S(2)}) %collective-permute-start.8) | collective-permute-done | bytes 65568 | tf_op jit(solution)/shard_map/ppermute | solution.py:55
  94.6 0.8 collective-permute-start.12
  95.4 4.5 %collective-permute-start.17 = (bf16[64,512]{1,0:T(8,128)(2,1)S(1)}, bf16[64,512]{1,0:T(8,128)(2,1)S(1)}, u32[]{:S(2)}, u32[]{:S(2)}) collective-permute-start(bf16[64,512]{1,0:T(8,128)(2,1)S(1)} %get-tuple-element.12), channel_id=1, source_target_pairs={{0,16},{8,24},{16,0},{24,8},{1,17},{9,25},{17,1},{25,9},{2,18},{10... | collective-permute-start | bytes 196616 | tf_op jit(solution)/shard_map/ppermute | solution.py:55
  99.9 1.6 collective-permute-done.16
  101.5 2.3 %collective-permute-done.17 = bf16[64,512]{1,0:T(8,128)(2,1)S(1)} collective-permute-done((bf16[64,512]{1,0:T(8,128)(2,1)S(1)}, bf16[64,512]{1,0:T(8,128)(2,1)S(1)}, u32[]{:S(2)}, u32[]{:S(2)}) %collective-permute-start.17) | collective-permute-done | bytes 65568 | tf_op jit(solution)/shard_map/ppermute | solution.py:55
  103.8 1.0 collective-permute-done.18
  104.8 2.1 %fusion.19 = bf16[64,256]{1,0:T(8,128)(2,1)S(1)} fusion(bf16[64,2048]{1,0:T(8,128)(2,1)S(1)} %constant_dynamic-update-slice_fusion.15, bf16[256,2048]{1,0:T(8,128)(2,1)} %collective-permute-done.3, pred[]{:T(512)S(6)} %eq.5, bf16[1,256,2048]{2,1,0:T(8,128)(2,1)} %param.10), kind=kOutput, calls=%fused_computation.41 | convolution fusion | flops 67633152 | bytes 2392065 | tf_op jit(solution)/shard_map/dot_general | solution.py:69
  106.9 1.7 select_convert_fusion.1
  108.7 18.6 %collective-permute-start.19 = (bf16[64,512]{1,0:T(8,128)(2,1)S(1)}, bf16[64,512]{1,0:T(8,128)(2,1)S(1)}, u32[]{:S(2)}, u32[]{:S(2)}) collective-permute-start(bf16[64,512]{1,0:T(8,128)(2,1)S(1)} %pad_maximum_fusion.4), channel_id=1, source_target_pairs={{0,2},{1,3},{4,6},{5,7},{8,10},{9,11},{12,14},{13,15},{16,18},{17,... | collective-permute-start | bytes 196616 | tf_op jit(solution)/shard_map/ppermute | solution.py:27
  127.6 1.3 collective-permute-start.9
  128.9 0.8 collective-permute-done.19
  129.7 1.5 collective-permute-start.20
  131.3 2.7 %collective-permute-start.21 = (bf16[64,512]{1,0:T(8,128)(2,1)S(1)}, bf16[64,512]{1,0:T(8,128)(2,1)S(1)}, u32[]{:S(2)}, u32[]{:S(2)}) collective-permute-start(bf16[64,512]{1,0:T(8,128)(2,1)S(1)} %collective-permute-done.19), channel_id=1, source_target_pairs={{0,16},{8,24},{16,0},{24,8},{1,17},{9,25},{17,1},{25,9},{2,18},{10... | collective-permute-start | bytes 196616 | tf_op jit(solution)/shard_map/ppermute | solution.py:55
  134.0 1.8 collective-permute-done.20
  135.8 1.4 collective-permute-done.21
  137.2 1.1 collective-permute-done.22
  138.3 1.9 %broadcast_select_fusion = (bf16[2,256,2048]{2,1,0:T(8,128)(2,1)S(1)}, bf16[2,256,2048]{2,1,0:T(8,128)(2,1)S(1)}) fusion(bf16[2,256,2048]{2,1,0:T(8,128)(2,1)S(1)} %collective-permute-done.12, bf16[2,256,2048]{2,1,0:T(8,128)(2,1)} %collective-permute-done.11, pred[]{:T(512)S(6)} %eq.5), kind=kLoop, calls=%fused_computation.3 | loop fusion | flops 2097152 | bytes 8388609 | tf_op jit(solution)/shard_map/jit(_where)/select_n | solution.py:79
  140.6 0.5 broadcast_select_fusion.33
  141.5 0.4 broadcast_select_fusion.37
  142.3 2.9 %collective-permute-start.24 = (bf16[64,512]{1,0:T(8,128)(2,1)S(1)}, bf16[64,512]{1,0:T(8,128)(2,1)S(1)}, u32[]{:S(2)}, u32[]{:S(2)}) collective-permute-start(bf16[64,512]{1,0:T(8,128)(2,1)S(1)} %get-tuple-element.10), channel_id=1, source_target_pairs={{0,16},{8,24},{16,0},{24,8},{1,17},{9,25},{17,1},{25,9},{2,18},{10... | collective-permute-start | bytes 196616 | tf_op jit(solution)/shard_map/ppermute | solution.py:55
  145.1 0.8 collective-permute-start.25
  146.4 0.5 broadcast_select_fusion.27
  147.3 0.9 collective-permute-done.23
  148.2 1.2 collective-permute-done.25
  149.4 1.7 fusion.10
  151.1 0.5 broadcast_select_fusion.31
  151.6 1.4 collective-permute-start.26
  153.4 2.9 %collective-permute-start.27 = (bf16[64,512]{1,0:T(8,128)(2,1)S(1)}, bf16[64,512]{1,0:T(8,128)(2,1)S(1)}, u32[]{:S(2)}, u32[]{:S(2)}) collective-permute-start(bf16[64,512]{1,0:T(8,128)(2,1)S(1)} %get-tuple-element.8), channel_id=1, source_target_pairs={{0,16},{8,24},{16,0},{24,8},{1,17},{9,25},{17,1},{25,9},{2,18},{10... | collective-permute-start | bytes 196616 | tf_op jit(solution)/shard_map/ppermute | solution.py:55
  156.3 1.4 collective-permute-done.26
  157.7 1.4 collective-permute-done.27
  159.2 2.6 %collective-permute-done.28 = bf16[64,512]{1,0:T(8,128)(2,1)S(1)} collective-permute-done((bf16[64,512]{1,0:T(8,128)(2,1)S(1)}, bf16[64,512]{1,0:T(8,128)(2,1)S(1)}, u32[]{:S(2)}, u32[]{:S(2)}) %collective-permute-start.28) | collective-permute-done | bytes 65568 | tf_op jit(solution)/shard_map/ppermute | solution.py:55
  162.9 2.3 %collective-permute-start.30 = (bf16[64,512]{1,0:T(8,128)(2,1)S(1)}, bf16[64,512]{1,0:T(8,128)(2,1)S(1)}, u32[]{:S(2)}, u32[]{:S(2)}) collective-permute-start(bf16[64,512]{1,0:T(8,128)(2,1)S(1)} %get-tuple-element.6), channel_id=1, source_target_pairs={{0,16},{8,24},{16,0},{24,8},{1,17},{9,25},{17,1},{25,9},{2,18},{10... | collective-permute-start | bytes 196616 | tf_op jit(solution)/shard_map/ppermute | solution.py:55
  165.2 1.7 collective-permute-start.31
  166.9 2.0 %collective-permute-done.29 = bf16[64,512]{1,0:T(8,128)(2,1)S(1)} collective-permute-done((bf16[64,512]{1,0:T(8,128)(2,1)S(1)}, bf16[64,512]{1,0:T(8,128)(2,1)S(1)}, u32[]{:S(2)}, u32[]{:S(2)}) %collective-permute-start.29) | collective-permute-done | bytes 65568 | tf_op jit(solution)/shard_map/ppermute | solution.py:55
  168.9 0.7 collective-permute-done.31
  169.6 2.0 %fusion.18 = f32[64,256]{1,0:T(8,128)S(1)} fusion(bf16[64,2048]{1,0:T(8,128)(2,1)S(1)} %constant_dynamic-update-slice_fusion.27, bf16[256,2048]{1,0:T(8,128)(2,1)} %collective-permute-done.3, pred[]{:T(512)S(6)} %eq.5, bf16[1,256,2048]{2,1,0:T(8,128)(2,1)} %param.10), kind=kOutput, calls=%fused_computation.40 | convolution fusion | flops 67633152 | bytes 2424833 | tf_op jit(solution)/shard_map/dot_general | solution.py:69
  171.6 1.7 broadcast_select_fusion.23
  173.5 8.4 %all_to_all.10 = f32[4,64,256]{2,1,0:T(8,128)S(1)} all-to-all(f32[4,64,256]{2,1,0:T(8,128)S(1)} %bitcast.115), channel_id=1, replica_groups=mesh['cz'=4,'cy'=2,'rx'=2,'rc'=2] {'cy','rc'}, dimensions={0} | all-to-all | bytes 524288 | tf_op jit(solution)/shard_map/all_to_all | solution.py:138
  181.9 0.8 copy.12
  (83 shorter events, 6.0 us)
Async XLA Ops:
  0.0 0.7 copy-start
  10.4 44.8 %all-to-all-start = ((bf16[16,64,512]{2,1,0:T(8,128)(2,1)}), bf16[16,64,512]{2,1,0:T(8,128)(2,1)S(1)}, u32[]{:S(2)}, u32[]{:S(2)}) async-start(bf16[16,64,512]{2,1,0:T(8,128)(2,1)} %bitcast.3), calls=%async_computation | async-start | bytes 2097152 | tf_op jit(solution)/shard_map/all_to_all | solution.py:114
  17.8 37.4 %collective-permute-start.4 = (bf16[256,2048]{1,0:T(8,128)(2,1)}, bf16[256,2048]{1,0:T(8,128)(2,1)S(1)}, u32[]{:S(2)}, u32[]{:S(2)}) collective-permute-start(bf16[256,2048]{1,0:T(8,128)(2,1)} %bitcast.6), channel_id=1, source_target_pairs={{0,4},{1,5},{2,6},{3,7},{4,0},{5,1},{6,2},{7,3},{8,12},{9,13},{10,... | collective-permute-start | bytes 3145736 | tf_op jit(solution)/shard_map/ppermute | solution.py:27
  19.7 54.5 %collective-permute-start.3 = (bf16[256,2048]{1,0:T(8,128)(2,1)}, bf16[256,2048]{1,0:T(8,128)(2,1)}, u32[]{:S(2)}, u32[]{:S(2)}) collective-permute-start(bf16[256,2048]{1,0:T(8,128)(2,1)} %bitcast.6), channel_id=1, source_target_pairs={{0,1},{1,0},{2,3},{3,2},{4,5},{5,4},{6,7},{7,6},{8,9},{9,8},{10,11... | collective-permute-start | bytes 3145736 | tf_op jit(solution)/shard_map/ppermute | solution.py:27
  21.1 50.0 %collective-permute-start.14 = (bf16[256,2048]{1,0:T(8,128)(2,1)S(1)}, bf16[256,2048]{1,0:T(8,128)(2,1)}, u32[]{:S(2)}, u32[]{:S(2)}) collective-permute-start(bf16[256,2048]{1,0:T(8,128)(2,1)S(1)} %dynamic-slice_bitcast_fusion), channel_id=1, source_target_pairs={{1,5},{3,7},{5,1},{7,3},{9,13},{11,15},{13,9},{15,11},{17,21},{19,... | collective-permute-start | bytes 3145736 | tf_op jit(solution)/shard_map/ppermute | solution.py:27
  55.2 20.7 %collective-permute-start.5 = (bf16[256,2048]{1,0:T(8,128)(2,1)S(1)}, bf16[256,2048]{1,0:T(8,128)(2,1)}, u32[]{:S(2)}, u32[]{:S(2)}) collective-permute-start(bf16[256,2048]{1,0:T(8,128)(2,1)S(1)} %collective-permute-done.4), channel_id=1, source_target_pairs={{0,1},{1,0},{2,3},{3,2},{4,5},{5,4},{6,7},{7,6},{8,9},{9,8},{10,11... | collective-permute-start | bytes 3145736 | tf_op jit(solution)/shard_map/ppermute | solution.py:27
  55.4 6.7 %collective-permute-start = (bf16[64,512]{1,0:T(8,128)(2,1)S(1)}, bf16[64,512]{1,0:T(8,128)(2,1)S(1)}, u32[]{:S(2)}, u32[]{:S(2)}) collective-permute-start(bf16[64,512]{1,0:T(8,128)(2,1)S(1)} %get-tuple-element.14), channel_id=1, source_target_pairs={{0,8},{8,16},{16,24},{24,0},{1,9},{9,17},{17,25},{25,1},{2,10},{10... | collective-permute-start | bytes 196616 | tf_op jit(solution)/shard_map/ppermute | solution.py:55
  60.1 34.5 %collective-permute-start.11 = (bf16[2,256,2048]{2,1,0:T(8,128)(2,1)}, bf16[2,256,2048]{2,1,0:T(8,128)(2,1)}, u32[]{:S(2)}, u32[]{:S(2)}) collective-permute-start(bf16[2,256,2048]{2,1,0:T(8,128)(2,1)} %slice_bitcast_fusion), channel_id=1, source_target_pairs={{2,6},{3,7},{6,2},{7,3},{10,14},{11,15},{14,10},{15,11},{18,22},{1... | collective-permute-start | bytes 6291464 | tf_op jit(solution)/shard_map/ppermute | solution.py:27
  62.1 6.6 %collective-permute-start.1 = (bf16[64,512]{1,0:T(8,128)(2,1)S(1)}, bf16[64,512]{1,0:T(8,128)(2,1)S(1)}, u32[]{:S(2)}, u32[]{:S(2)}) collective-permute-start(bf16[64,512]{1,0:T(8,128)(2,1)S(1)} %get-tuple-element.14), channel_id=1, source_target_pairs={{0,16},{8,24},{16,0},{24,8},{1,17},{9,25},{17,1},{25,9},{2,18},{10... | collective-permute-start | bytes 196616 | tf_op jit(solution)/shard_map/ppermute | solution.py:55
  68.6 4.3 %collective-permute-start.2 = (bf16[64,512]{1,0:T(8,128)(2,1)S(1)}, bf16[64,512]{1,0:T(8,128)(2,1)S(1)}, u32[]{:S(2)}, u32[]{:S(2)}) collective-permute-start(bf16[64,512]{1,0:T(8,128)(2,1)S(1)} %get-tuple-element.14), channel_id=1, source_target_pairs={{0,24},{8,0},{16,8},{24,16},{1,25},{9,1},{17,9},{25,17},{2,26},{10... | collective-permute-start | bytes 196616 | tf_op jit(solution)/shard_map/ppermute | solution.py:55
  71.0 22.5 %collective-permute-start.13 = (bf16[256,2048]{1,0:T(8,128)(2,1)S(1)}, bf16[256,2048]{1,0:T(8,128)(2,1)S(1)}, u32[]{:S(2)}, u32[]{:S(2)}) collective-permute-start(bf16[256,2048]{1,0:T(8,128)(2,1)S(1)} %dynamic-slice_bitcast_fusion), channel_id=1, source_target_pairs={{1,0},{3,2},{5,4},{7,6},{9,8},{11,10},{13,12},{15,14},{17,16},{19,... | collective-permute-start | bytes 3145736 | tf_op jit(solution)/shard_map/ppermute | solution.py:27
  72.9 21.1 %collective-permute-start.15 = (bf16[256,2048]{1,0:T(8,128)(2,1)}, bf16[256,2048]{1,0:T(8,128)(2,1)S(1)}, u32[]{:S(2)}, u32[]{:S(2)}) collective-permute-start(bf16[256,2048]{1,0:T(8,128)(2,1)} %collective-permute-done.14), channel_id=1, source_target_pairs={{1,0},{3,2},{5,4},{7,6},{9,8},{11,10},{13,12},{15,14},{17,16},{19,... | collective-permute-start | bytes 3145736 | tf_op jit(solution)/shard_map/ppermute | solution.py:27
  76.4 6.5 %collective-permute-start.6 = (bf16[64,512]{1,0:T(8,128)(2,1)S(1)}, bf16[64,512]{1,0:T(8,128)(2,1)S(1)}, u32[]{:S(2)}, u32[]{:S(2)}) collective-permute-start(bf16[64,512]{1,0:T(8,128)(2,1)S(1)} %get-tuple-element.37), channel_id=1, source_target_pairs={{0,8},{8,16},{16,24},{24,0},{1,9},{9,17},{17,25},{25,1},{2,10},{10... | collective-permute-start | bytes 196616 | tf_op jit(solution)/shard_map/ppermute | solution.py:55
  76.6 50.7 %collective-permute-start.10 = (bf16[2,256,2048]{2,1,0:T(8,128)(2,1)}, bf16[2,256,2048]{2,1,0:T(8,128)(2,1)S(1)}, u32[]{:S(2)}, u32[]{:S(2)}) collective-permute-start(bf16[2,256,2048]{2,1,0:T(8,128)(2,1)} %slice_bitcast_fusion), channel_id=1, source_target_pairs={{2,3},{3,2},{6,7},{7,6},{10,11},{11,10},{14,15},{15,14},{18,19},{1... | collective-permute-start | bytes 6291464 | tf_op jit(solution)/shard_map/ppermute | solution.py:27
  82.9 6.3 %collective-permute-start.7 = (bf16[64,512]{1,0:T(8,128)(2,1)S(1)}, bf16[64,512]{1,0:T(8,128)(2,1)S(1)}, u32[]{:S(2)}, u32[]{:S(2)}) collective-permute-start(bf16[64,512]{1,0:T(8,128)(2,1)S(1)} %get-tuple-element.37), channel_id=1, source_target_pairs={{0,16},{8,24},{16,0},{24,8},{1,17},{9,25},{17,1},{25,9},{2,18},{10... | collective-permute-start | bytes 196616 | tf_op jit(solution)/shard_map/ppermute | solution.py:55
  89.2 4.3 %collective-permute-start.8 = (bf16[64,512]{1,0:T(8,128)(2,1)S(1)}, bf16[64,512]{1,0:T(8,128)(2,1)S(1)}, u32[]{:S(2)}, u32[]{:S(2)}) collective-permute-start(bf16[64,512]{1,0:T(8,128)(2,1)S(1)} %get-tuple-element.37), channel_id=1, source_target_pairs={{0,24},{8,0},{16,8},{24,16},{1,25},{9,1},{17,9},{25,17},{2,26},{10... | collective-permute-start | bytes 196616 | tf_op jit(solution)/shard_map/ppermute | solution.py:55
  94.5 7.0 %collective-permute-start.16 = (bf16[64,512]{1,0:T(8,128)(2,1)S(1)}, bf16[64,512]{1,0:T(8,128)(2,1)S(1)}, u32[]{:S(2)}, u32[]{:S(2)}) collective-permute-start(bf16[64,512]{1,0:T(8,128)(2,1)S(1)} %get-tuple-element.12), channel_id=1, source_target_pairs={{0,8},{8,16},{16,24},{24,0},{1,9},{9,17},{17,25},{25,1},{2,10},{10... | collective-permute-start | bytes 196616 | tf_op jit(solution)/shard_map/ppermute | solution.py:55
  94.6 43.7 %collective-permute-start.12 = (bf16[2,256,2048]{2,1,0:T(8,128)(2,1)}, bf16[2,256,2048]{2,1,0:T(8,128)(2,1)S(1)}, u32[]{:S(2)}, u32[]{:S(2)}) collective-permute-start(bf16[2,256,2048]{2,1,0:T(8,128)(2,1)} %collective-permute-done.11), channel_id=1, source_target_pairs={{2,3},{3,2},{6,7},{7,6},{10,11},{11,10},{14,15},{15,14},{18,19},{1... | collective-permute-start | bytes 6291464 | tf_op jit(solution)/shard_map/ppermute | solution.py:27
  95.4 8.4 %collective-permute-start.17 = (bf16[64,512]{1,0:T(8,128)(2,1)S(1)}, bf16[64,512]{1,0:T(8,128)(2,1)S(1)}, u32[]{:S(2)}, u32[]{:S(2)}) collective-permute-start(bf16[64,512]{1,0:T(8,128)(2,1)S(1)} %get-tuple-element.12), channel_id=1, source_target_pairs={{0,16},{8,24},{16,0},{24,8},{1,17},{9,25},{17,1},{25,9},{2,18},{10... | collective-permute-start | bytes 196616 | tf_op jit(solution)/shard_map/ppermute | solution.py:55
  99.8 4.9 %collective-permute-start.18 = (bf16[64,512]{1,0:T(8,128)(2,1)S(1)}, bf16[64,512]{1,0:T(8,128)(2,1)S(1)}, u32[]{:S(2)}, u32[]{:S(2)}) collective-permute-start(bf16[64,512]{1,0:T(8,128)(2,1)S(1)} %get-tuple-element.12), channel_id=1, source_target_pairs={{0,24},{8,0},{16,8},{24,16},{1,25},{9,1},{17,9},{25,17},{2,26},{10... | collective-permute-start | bytes 196616 | tf_op jit(solution)/shard_map/ppermute | solution.py:55
  104.8 22.5 %copy-start.1 = (bf16[1,4,256,2048]{3,2,1,0:T(8,128)(2,1)S(1)}, bf16[1,4,256,2048]{3,2,1,0:T(8,128)(2,1)}, u32[]{:S(2)}) copy-start(bf16[1,4,256,2048]{3,2,1,0:T(8,128)(2,1)} %param.11) | copy-start | bytes 12582916
  108.7 21.1 %collective-permute-start.19 = (bf16[64,512]{1,0:T(8,128)(2,1)S(1)}, bf16[64,512]{1,0:T(8,128)(2,1)S(1)}, u32[]{:S(2)}, u32[]{:S(2)}) collective-permute-start(bf16[64,512]{1,0:T(8,128)(2,1)S(1)} %pad_maximum_fusion.4), channel_id=1, source_target_pairs={{0,2},{1,3},{4,6},{5,7},{8,10},{9,11},{12,14},{13,15},{16,18},{17,... | collective-permute-start | bytes 196616 | tf_op jit(solution)/shard_map/ppermute | solution.py:27
  127.6 13.5 %collective-permute-start.9 = (bf16[64,2048]{1,0:T(8,128)(2,1)S(1)}, bf16[64,2048]{1,0:T(8,128)(2,1)S(1)}, u32[]{:S(2)}, u32[]{:S(2)}) collective-permute-start(bf16[64,2048]{1,0:T(8,128)(2,1)S(1)} %constant_dynamic-update-slice_fusion.19), channel_id=1, source_target_pairs={{0,2},{1,3},{4,6},{5,7},{8,10},{9,11},{12,14},{13,15},{16,18},{17,... | collective-permute-start | bytes 786440 | tf_op jit(solution)/shard_map/ppermute | solution.py:27
  129.7 6.1 %collective-permute-start.20 = (bf16[64,512]{1,0:T(8,128)(2,1)S(1)}, bf16[64,512]{1,0:T(8,128)(2,1)S(1)}, u32[]{:S(2)}, u32[]{:S(2)}) collective-permute-start(bf16[64,512]{1,0:T(8,128)(2,1)S(1)} %collective-permute-done.19), channel_id=1, source_target_pairs={{0,8},{8,16},{16,24},{24,0},{1,9},{9,17},{17,25},{25,1},{2,10},{10... | collective-permute-start | bytes 196616 | tf_op jit(solution)/shard_map/ppermute | solution.py:55
  131.3 5.9 %collective-permute-start.21 = (bf16[64,512]{1,0:T(8,128)(2,1)S(1)}, bf16[64,512]{1,0:T(8,128)(2,1)S(1)}, u32[]{:S(2)}, u32[]{:S(2)}) collective-permute-start(bf16[64,512]{1,0:T(8,128)(2,1)S(1)} %collective-permute-done.19), channel_id=1, source_target_pairs={{0,16},{8,24},{16,0},{24,8},{1,17},{9,25},{17,1},{25,9},{2,18},{10... | collective-permute-start | bytes 196616 | tf_op jit(solution)/shard_map/ppermute | solution.py:55
  134.0 4.3 %collective-permute-start.22 = (bf16[64,512]{1,0:T(8,128)(2,1)S(1)}, bf16[64,512]{1,0:T(8,128)(2,1)S(1)}, u32[]{:S(2)}, u32[]{:S(2)}) collective-permute-start(bf16[64,512]{1,0:T(8,128)(2,1)S(1)} %collective-permute-done.19), channel_id=1, source_target_pairs={{0,24},{8,0},{16,8},{24,16},{1,25},{9,1},{17,9},{25,17},{2,26},{10... | collective-permute-start | bytes 196616 | tf_op jit(solution)/shard_map/ppermute | solution.py:55
  142.0 6.1 %collective-permute-start.23 = (bf16[64,512]{1,0:T(8,128)(2,1)S(1)}, bf16[64,512]{1,0:T(8,128)(2,1)S(1)}, u32[]{:S(2)}, u32[]{:S(2)}) collective-permute-start(bf16[64,512]{1,0:T(8,128)(2,1)S(1)} %get-tuple-element.10), channel_id=1, source_target_pairs={{0,8},{8,16},{16,24},{24,0},{1,9},{9,17},{17,25},{25,1},{2,10},{10... | collective-permute-start | bytes 196616 | tf_op jit(solution)/shard_map/ppermute | solution.py:55
  142.3 5.9 %collective-permute-start.24 = (bf16[64,512]{1,0:T(8,128)(2,1)S(1)}, bf16[64,512]{1,0:T(8,128)(2,1)S(1)}, u32[]{:S(2)}, u32[]{:S(2)}) collective-permute-start(bf16[64,512]{1,0:T(8,128)(2,1)S(1)} %get-tuple-element.10), channel_id=1, source_target_pairs={{0,16},{8,24},{16,0},{24,8},{1,17},{9,25},{17,1},{25,9},{2,18},{10... | collective-permute-start | bytes 196616 | tf_op jit(solution)/shard_map/ppermute | solution.py:55
  145.1 4.3 %collective-permute-start.25 = (bf16[64,512]{1,0:T(8,128)(2,1)S(1)}, bf16[64,512]{1,0:T(8,128)(2,1)S(1)}, u32[]{:S(2)}, u32[]{:S(2)}) collective-permute-start(bf16[64,512]{1,0:T(8,128)(2,1)S(1)} %get-tuple-element.10), channel_id=1, source_target_pairs={{0,24},{8,0},{16,8},{24,16},{1,25},{9,1},{17,9},{25,17},{2,26},{10... | collective-permute-start | bytes 196616 | tf_op jit(solution)/shard_map/ppermute | solution.py:55
  151.6 6.1 %collective-permute-start.26 = (bf16[64,512]{1,0:T(8,128)(2,1)S(1)}, bf16[64,512]{1,0:T(8,128)(2,1)S(1)}, u32[]{:S(2)}, u32[]{:S(2)}) collective-permute-start(bf16[64,512]{1,0:T(8,128)(2,1)S(1)} %get-tuple-element.8), channel_id=1, source_target_pairs={{0,8},{8,16},{16,24},{24,0},{1,9},{9,17},{17,25},{25,1},{2,10},{10... | collective-permute-start | bytes 196616 | tf_op jit(solution)/shard_map/ppermute | solution.py:55
  153.4 5.7 %collective-permute-start.27 = (bf16[64,512]{1,0:T(8,128)(2,1)S(1)}, bf16[64,512]{1,0:T(8,128)(2,1)S(1)}, u32[]{:S(2)}, u32[]{:S(2)}) collective-permute-start(bf16[64,512]{1,0:T(8,128)(2,1)S(1)} %get-tuple-element.8), channel_id=1, source_target_pairs={{0,16},{8,24},{16,0},{24,8},{1,17},{9,25},{17,1},{25,9},{2,18},{10... | collective-permute-start | bytes 196616 | tf_op jit(solution)/shard_map/ppermute | solution.py:55
  156.3 5.5 %collective-permute-start.28 = (bf16[64,512]{1,0:T(8,128)(2,1)S(1)}, bf16[64,512]{1,0:T(8,128)(2,1)S(1)}, u32[]{:S(2)}, u32[]{:S(2)}) collective-permute-start(bf16[64,512]{1,0:T(8,128)(2,1)S(1)} %get-tuple-element.8), channel_id=1, source_target_pairs={{0,24},{8,0},{16,8},{24,16},{1,25},{9,1},{17,9},{25,17},{2,26},{10... | collective-permute-start | bytes 196616 | tf_op jit(solution)/shard_map/ppermute | solution.py:55
  162.7 6.1 %collective-permute-start.29 = (bf16[64,512]{1,0:T(8,128)(2,1)S(1)}, bf16[64,512]{1,0:T(8,128)(2,1)S(1)}, u32[]{:S(2)}, u32[]{:S(2)}) collective-permute-start(bf16[64,512]{1,0:T(8,128)(2,1)S(1)} %get-tuple-element.6), channel_id=1, source_target_pairs={{0,8},{8,16},{16,24},{24,0},{1,9},{9,17},{17,25},{25,1},{2,10},{10... | collective-permute-start | bytes 196616 | tf_op jit(solution)/shard_map/ppermute | solution.py:55
  162.9 5.9 %collective-permute-start.30 = (bf16[64,512]{1,0:T(8,128)(2,1)S(1)}, bf16[64,512]{1,0:T(8,128)(2,1)S(1)}, u32[]{:S(2)}, u32[]{:S(2)}) collective-permute-start(bf16[64,512]{1,0:T(8,128)(2,1)S(1)} %get-tuple-element.6), channel_id=1, source_target_pairs={{0,16},{8,24},{16,0},{24,8},{1,17},{9,25},{17,1},{25,9},{2,18},{10... | collective-permute-start | bytes 196616 | tf_op jit(solution)/shard_map/ppermute | solution.py:55
  165.2 4.4 %collective-permute-start.31 = (bf16[64,512]{1,0:T(8,128)(2,1)S(1)}, bf16[64,512]{1,0:T(8,128)(2,1)S(1)}, u32[]{:S(2)}, u32[]{:S(2)}) collective-permute-start(bf16[64,512]{1,0:T(8,128)(2,1)S(1)} %get-tuple-element.6), channel_id=1, source_target_pairs={{0,24},{8,0},{16,8},{24,16},{1,25},{9,1},{17,9},{25,17},{2,26},{10... | collective-permute-start | bytes 196616 | tf_op jit(solution)/shard_map/ppermute | solution.py:55

commit v2 on v1

v2 whole, which is shorter than its diff:
```python
import jax
import jax.numpy as jnp
from jax import lax
from jax.experimental import pallas as pl
from jax.experimental.pallas import tpu as pltpu
from jax.sharding import Mesh, PartitionSpec as P

AXES = ("cz", "cy", "rx", "rc")


def solution(mesh):
    cols, rows = mesh.shape["col"], mesh.shape["row"]
    sizes = (cols // 2, 2, rows // 2, 2)
    grid = Mesh(mesh.devices.reshape(sizes), AXES)
    count_z, _, count_x, _ = sizes
    bf16 = jnp.bfloat16

    def place(z, y, x, c):
        return ((z * 2 + y) * sizes[2] + x) * 2 + c

    def send(value, target, only=None):
        pairs = []
        for z in range(sizes[0]):
            for y in range(2):
                for x in range(sizes[2]):
                    for c in range(2):
                        if only is None or only(z, y, x, c):
                            pairs.append((place(z, y, x, c), place(*target(z, y, x, c))))
        return lax.ppermute(value, AXES, pairs)

    def over_y(z, y, x, c):
        return z, 1 - y, x, c

    def over_core(z, y, x, c):
        return z, y, x, 1 - c

    def over_both(z, y, x, c):
        return z, 1 - y, x, 1 - c

    def picked(flag, why, vector, own, own_y, other, other_y, index):
        part, depth = vector.shape
        each = own.shape[1]

        def kernel(flags, vector_ref, own_ref, own_y_ref, other_ref, other_y_ref, out_ref, held, sems):
            def copies(first, second):
                return [
                    pltpu.make_async_copy(ref.at[index], held.at[slot], sems.at[slot])
                    for slot, ref in enumerate((first, second))
                ]

            @pl.when(flags[0] == 0)
            def _():
                for copy in copies(own_ref, own_y_ref):
                    copy.start()

            @pl.when(flags[0] != 0)
            def _():
                for copy in copies(other_ref, other_y_ref):
                    copy.start()

            results = []
            for slot, copy in enumerate(copies(own_ref, own_y_ref)):
                copy.wait()
                results.append(
                    lax.dot_general(
                        held[slot], vector_ref[...], (((1,), (1,)), ((), ())),
                        preferred_element_type=jnp.float32,
                    ).T
                )
            first = flags[1] == 0
            out_ref[:, :each] = jnp.where(first, results[0], results[1])
            out_ref[:, each:] = jnp.where(first, results[1], results[0])

        whole = pl.BlockSpec(memory_space=pltpu.VMEM)
        far = pl.BlockSpec(memory_space=pl.ANY)
        return pl.pallas_call(
            kernel,
            in_specs=[pl.BlockSpec(memory_space=pltpu.SMEM), whole, far, far, far, far],
            out_specs=whole,
            scratch_shapes=[
                pltpu.VMEM((2, each, depth), bf16),
                pltpu.SemaphoreType.DMA((2,)),
            ],
            out_shape=jax.ShapeDtypeStruct((part, 2 * each), jnp.float32),
            cost_estimate=pl.CostEstimate(
                flops=4 * part * depth * each,
                bytes_accessed=4 * each * depth,
                transcendentals=0,
            ),
            compiler_params=pltpu.CompilerParams(vmem_limit_bytes=8 * 1024 * 1024),
        )(jnp.stack([flag, why]).astype(jnp.int32), vector, own, own_y, other, other_y)

    def prior_parts(zed, why, right_side, prior_solution, factor_codes, block_scale):
        each, width = right_side.shape
        panel, depth = factor_codes.shape
        blocks = block_scale.shape[1]
        deep = depth // blocks
        chunk = 2 * each

        rows = chunk
        split = chunk // rows

        def kernel(place_ref, scale_ref, right_ref, prior_ref, codes_ref, out_ref, scaled, total):
            step = pl.program_id(0)

            @pl.when(step == 0)
            def _():
                for b in range(blocks):
                    part = prior_ref[b * deep : (b + 1) * deep, :].astype(jnp.float32)
                    scaled[b * deep : (b + 1) * deep, :] = (part * scale_ref[0, b]).astype(bf16)

            total[...] = -jnp.dot(
                codes_ref[...], scaled[...], preferred_element_type=jnp.float32
            )

            @pl.when(step == (place_ref[0] * 2 + place_ref[1]) // (rows // each))
            def _():
                first = 0 if rows == each else pl.multiple_of(place_ref[1] * each, each)
                total[pl.ds(first, each), :] += right_ref[...]

            out_ref[0] = total[...].T.astype(bf16)

        return pl.pallas_call(
            kernel,
            grid_spec=pltpu.PrefetchScalarGridSpec(
                num_scalar_prefetch=1,
                grid=(panel // rows,),
                in_specs=[
                    pl.BlockSpec(memory_space=pltpu.SMEM),
                    pl.BlockSpec((each, width), lambda i, p: (0, 0)),
                    pl.BlockSpec((depth, width), lambda i, p: (0, 0)),
                    pl.BlockSpec((rows, depth), lambda i, p: (i, 0)),
                ],
                out_specs=pl.BlockSpec((1, width, rows), lambda i, p: (i // split, 0, i % split)),
                scratch_shapes=[
                    pltpu.VMEM((depth, width), bf16),
                    pltpu.VMEM((rows, width), jnp.float32),
                ],
            ),
            out_shape=jax.ShapeDtypeStruct((panel // chunk, width, chunk), bf16),
            cost_estimate=pl.CostEstimate(
                flops=2 * panel * depth * width,
                bytes_accessed=2 * panel * depth + 4 * panel * width,
                transcendentals=0,
            ),
            compiler_params=pltpu.CompilerParams(vmem_limit_bytes=60 * 1024 * 1024),
        )(jnp.stack([zed, why]).astype(jnp.int32), block_scale, right_side, prior_solution, factor_codes)

    def over_y(z, y, x, c):
        return z, 1 - y, x, c

    def over_core(z, y, x, c):
        return z, y, x, 1 - c

    def over_both(z, y, x, c):
        return z, 1 - y, x, 1 - c

    def picked(flag, why, vector, own, own_y, other, other_y, index):
        part, depth = vector.shape
        each = own.shape[1]

        def kernel(flags, vector_ref, own_ref, own_y_ref, other_ref, other_y_ref, out_ref, held, sems):
            def copies(first, second):
                return [
                    pltpu.make_async_copy(ref.at[index], held.at[slot], sems.at[slot])
                    for slot, ref in enumerate((first, second))
                ]

            @pl.when(flags[0] == 0)
            def _():
                for copy in copies(own_ref, own_y_ref):
                    copy.start()

            @pl.when(flags[0] != 0)
            def _():
                for copy in copies(other_ref, other_y_ref):
                    copy.start()

            results = []
            for slot, copy in enumerate(copies(own_ref, own_y_ref)):
                copy.wait()
                results.append(
                    lax.dot_general(
                        held[slot], vector_ref[...], (((1,), (1,)), ((), ())),
                        preferred_element_type=jnp.float32,
                    ).T
                )
            first = flags[1] == 0
            out_ref[:, :each] = jnp.where(first, results[0], results[1])
            out_ref[:, each:] = jnp.where(first, results[1], results[0])

        whole = pl.BlockSpec(memory_space=pltpu.VMEM)
        far = pl.BlockSpec(memory_space=pl.ANY)
        return pl.pallas_call(
            kernel,
            in_specs=[pl.BlockSpec(memory_space=pltpu.SMEM), whole, far, far, far, far],
            out_specs=whole,
            scratch_shapes=[
                pltpu.VMEM((2, each, depth), bf16),
                pltpu.SemaphoreType.DMA((2,)),
            ],
            out_shape=jax.ShapeDtypeStruct((part, 2 * each), jnp.float32),
            cost_estimate=pl.CostEstimate(
                flops=4 * part * depth * each,
                bytes_accessed=4 * each * depth,
                transcendentals=0,
            ),
            compiler_params=pltpu.CompilerParams(vmem_limit_bytes=8 * 1024 * 1024),
        )(jnp.stack([flag, why]).astype(jnp.int32), vector, own, own_y, other, other_y)

    def prior_parts(zed, why, right_side, prior_solution, factor_codes, block_scale):
        each, width = right_side.shape
        panel, depth = factor_codes.shape
        blocks = block_scale.shape[1]
        deep = depth // blocks
        chunk = 2 * each

        def kernel(place_ref, scale_ref, right_ref, prior_ref, codes_ref, out_ref, scaled, total):
            step = pl.program_id(0)

            @pl.when(step == 0)
            def _():
                for b in range(blocks):
                    part = prior_ref[b * deep : (b + 1) * deep, :].astype(jnp.float32)
                    scaled[b * deep : (b + 1) * deep, :] = (part * scale_ref[0, b]).astype(bf16)

            total[...] = -jnp.dot(
                codes_ref[...], scaled[...], preferred_element_type=jnp.float32
            )

            @pl.when(step == place_ref[0])
            def _():
                rows = pl.ds(pl.multiple_of(place_ref[1] * each, each), each)
                total[rows, :] += right_ref[...]

            out_ref[0] = total[...].T.astype(bf16)

        return pl.pallas_call(
            kernel,
            grid_spec=pltpu.PrefetchScalarGridSpec(
                num_scalar_prefetch=1,
                grid=(panel // chunk,),
                in_specs=[
                    pl.BlockSpec(memory_space=pltpu.SMEM),
                    pl.BlockSpec((each, width), lambda i, p: (0, 0)),
                    pl.BlockSpec((depth, width), lambda i, p: (0, 0)),
                    pl.BlockSpec((chunk, depth), lambda i, p: (i, 0)),
                ],
                out_specs=pl.BlockSpec((1, width, chunk), lambda i, p: (i, 0, 0)),
                scratch_shapes=[
                    pltpu.VMEM((depth, width), bf16),
                    pltpu.VMEM((chunk, width), jnp.float32),
                ],
            ),
            out_shape=jax.ShapeDtypeStruct((panel // chunk, width, chunk), bf16),
            cost_estimate=pl.CostEstimate(
                flops=2 * panel * depth * width,
                bytes_accessed=2 * panel * depth + 4 * panel * width,
                transcendentals=0,
            ),
            compiler_params=pltpu.CompilerParams(vmem_limit_bytes=60 * 1024 * 1024),
        )(jnp.stack([zed, why]).astype(jnp.int32), block_scale, right_side, prior_solution, factor_codes)

    def local(right_side, prior_solution, factor_codes, block_scale, diag_inverse, inner_factor):
        each, width = right_side.shape
        part = width // 4
        zed, why = lax.axis_index("cz"), lax.axis_index("cy")
        ex, core = lax.axis_index("rx"), lax.axis_index("rc")
        chunk = 2 * each
        panel = factor_codes.shape[0]

        def gather(piece):
            if count_z > 4:
                return jnp.moveaxis(lax.all_gather(piece, "cz", axis=0), 0, 1).reshape(part, panel)
            whole = jnp.zeros((part, panel), piece.dtype)
            got = [(zed, piece)]
            for step in range(1, count_z):

                def along(z, y, x, c):
                    return (z + step) % count_z, y, x, c

                moved = send(piece, along)
                got.append((lax.rem(zed + count_z - step, count_z), moved))
            for source, value in got:
                whole = lax.dynamic_update_slice(whole, value, (0, source * chunk))
            return whole

        def apply(pieces, vector):
            mine, beside = [
                lax.dot_general(
                    vector, piece, (((1,), (1,)), ((), ())), preferred_element_type=jnp.float32
                )
                for piece in pieces
            ]
            first = jnp.where(why == 0, mine, beside)
            second = jnp.where(why == 0, beside, mine)
            return jnp.concatenate([first, second], axis=1)

        def pick(even, odd):
            return lax.optimization_barrier(jnp.where(core == 0, even, odd))

        before = 2 * (count_x - 1)
        inverse = diag_inverse[0]
        turns = range(count_x)

        def odd_at(turn):
            return lambda z, y, x, c: x == turn and c == 1

        inverse_y = send(inverse, over_y)
        past = inner_factor[0, :before]
        past_y = send(past, over_y, lambda z, y, x, c: x > 0)
        pair = lax.dynamic_index_in_dim(inner_factor[0], 2 * ex, 0, keepdims=False)
        inverse_c = send(inverse, over_core)
        pair_c = send(pair, over_core)
        past_c = send(past, over_core)
        inverse_yc = send(inverse_y, over_core)
        past_yc = send(past_y, over_core)
        pair_y, pair_yc = {}, {}
        for turn in turns:
            pair_y[turn] = send(pair, over_y, odd_at(turn))
            pair_yc[turn] = send(pair_y[turn], over_core)
        inv_even = (pick(inverse, inverse_c), pick(inverse_y, inverse_yc))
        inv_odd = (pick(inverse_c, inverse), pick(inverse_yc, inverse_y))
        near_link = pick(pair_c, pair)
        link = {}
        for turn in turns:
            link[turn] = (near_link, pick(pair_yc[turn], pair_y[turn]))

        parts = prior_parts(zed, why, right_side, prior_solution, factor_codes, block_scale)
        parts = parts.reshape(count_z * 4, part, chunk)
        came = lax.all_to_all(parts, ("cz", "cy", "rc"), 0, 0)
        came = came.reshape(count_z * 2, 2, part, chunk).astype(jnp.float32).sum(0)
        rhs_even, rhs_odd = came[0], came[1]

        for turn in range(count_x):
            vector = gather(rhs_even.astype(bf16))
            even = apply(inv_even, vector)
            even_all = gather(even.astype(bf16))
            current = rhs_odd - apply(link[turn], even_all)
            vector = gather(current.astype(bf16))
            odd = apply(inv_odd, vector)
            kept = odd if turn == 0 else jnp.where(ex == turn, odd, kept)
            for later in range(turn + 1, count_x):

                def exchange(z, y, x, c):
                    return z, y, later if x == turn else turn if x == later else x, c

                seen_even = send(even_all, exchange)
                moved = send(odd.astype(bf16), exchange)
                seen_odd = gather(moved)
                here = ex == later
                for index, seen in ((2 * turn, seen_even), (2 * turn + 1, seen_odd)):
                    add = picked(core, why, seen, past, past_y, past_c, past_yc, index)
                    rhs_even = rhs_even - jnp.where(here, add, 0.0)
                    add = picked(1 - core, why, seen, past, past_y, past_c, past_yc, index)
                    rhs_odd = rhs_odd - jnp.where(here, add, 0.0)

        near = [jnp.where(why == 0, v[:, :each], v[:, each:]) for v in (even, kept)]
        far = [jnp.where(why == 0, v[:, each:], v[:, :each]) for v in (even, kept)]
        mine = jnp.where(core == 0, near[0], near[1])
        from_c = send(jnp.where(core == 0, near[1], near[0]), over_core)
        from_y = send(jnp.where(core == 0, far[0], far[1]), over_y)
        from_yc = send(jnp.where(core == 0, far[1], far[0]), over_both)
        by_y = [
            (jnp.where(core == 0, v, w), jnp.where(core == 0, w, v))
            for v, w in ((mine, from_c), (from_y, from_yc))
        ]
        blocks_out = [jnp.where(why == 0, v, w) for v, w in zip(by_y[0], by_y[1])]
        blocks_out += [jnp.where(why == 0, w, v) for v, w in zip(by_y[0], by_y[1])]
        return jnp.concatenate(blocks_out, axis=0).T

    return jax.shard_map(
        local,
        mesh=grid,
        in_specs=(
            P(("rx", "rc", "cz", "cy"), None),
            P(("cz", "cy"), None),
            P(("rx", "rc"), ("cz", "cy")),
            P(("rx", "rc"), ("cz", "cy")),
            P(("rx", "rc"), ("cz", "cy"), None),
            P(("rx", "rc"), None, ("cz", "cy"), None),
        ),
        out_specs=P(("rx", "rc", "cz", "cy"), None),
        check_vma=False,
    )
```

time: 184 us -> 183 us (level)
  Pallas kernels: 0 us -> 19.6 us
  matrix products: 23.6 us -> 7.6 us
  blocking collectives: 8.39 us -> 0 us
  other arithmetic: 2.51 us -> 10.5 us
    ppermute x21 -> x0, waiting for transfers between devices: 37.9 us -> none  [gather(): lax.ppermute(piece, 'cz', [(i, (i + step) % count_z) for i in range(count...]
    ppermute x11 -> x37, waiting for transfers between devices: 33.3 us -> 70.1 us  [send(): return lax.ppermute(value, AXES, pairs)]
    ppermute x21 -> x0, starting transfers between devices: 29.7 us -> none  [gather(): lax.ppermute(piece, 'cz', [(i, (i + step) % count_z) for i in range(count...]
    ppermute x11 -> x37, starting transfers between devices: 29.6 us -> 57.5 us  [send(): return lax.ppermute(value, AXES, pairs)]
    pallas_call x0 -> x5, Pallas kernels: none -> 19.6 us  [the longest x4 11.7 us: picked(): pl.pallas_call(kernel, in_specs=[pl.BlockSpec(memory_space=pltpu.SMEM), w...]
    dot_general x20 -> x12, matrix products: 17.1 us -> 7.6 us  [apply(): lax.dot_general(vector, piece, (((1,), (1,)), ((), ())), preferred_elemen...]
    all_to_all x1 -> x0, blocking collectives: 8.39 us -> none  [local(): out = lax.all_to_all(out.reshape(4, part, each), ('cy', 'rc'), 0, 0)]
    dot_general x1 -> x0, matrix products: 6.47 us -> none  [local(): lax.dot_general(scaled, factor_codes, (((0,), (1,)), ((), ())), preferred...]
  transfers between devices with their start and end apart: 33 -> 38, of which waited for: 20 -> 22; matrix products, arithmetic and copies ran while one was open for 9% -> 12% of each run, Pallas kernels for 0% -> 6%
where the time goes in v2:
time: 183 us; the launch traced here: 181 us
  waiting for transfers between devices  70.1 us (38%)
  starting transfers between devices  65.1 us (36%)
  Pallas kernels  19.6 us (11%)
  other arithmetic  10.5 us (6%)
  local copies, waits for them, and re-layouts  7.94 us (4%)
  matrix products  7.6 us (4%)
    ppermute x37, waiting for transfers between devices, send(): return lax.ppermute(value, AXES, pairs)  70.1 us
    ppermute x37, starting transfers between devices, send(): return lax.ppermute(value, AXES, pairs)  57.5 us
    pallas_call x4, Pallas kernels, picked(): pl.pallas_call(kernel, in_specs=[pl.BlockSpec(memory_space=pltpu.SMEM), w...  11.7 us
    pallas_call x1, Pallas kernels, prior_parts(): pl.pallas_call(kernel, grid_spec=pltpu.PrefetchScalarGridSpec(num_scalar_...  7.99 us
    dot_general x12, matrix products, apply(): lax.dot_general(vector, piece, (((1,), (1,)), ((), ())), preferred_elemen...  7.6 us
    all_to_all x1, starting transfers between devices, local(): came = lax.all_to_all(parts, ('cz', 'cy', 'rc'), 0, 0)  7.6 us
    select_n x5, other arithmetic, pick(): return lax.optimization_barrier(jnp.where(core == 0, even, odd))  7.4 us
  transfers between devices with their start and end apart: 38, of which 22 were waited for; matrix products, arithmetic and copies ran while one was open for 12% of the time, Pallas kernels for 6%

profile of v2, /device:TPU:0, one launch (start us, length us, event | category | flops | bytes accessed | tf_op | source)
XLA Modules:
  0.0 181.3 jit_solution(9001279536339480648)
XLA Ops:
  0.0 0.6 pad_add_fusion.place_ref
  0.6 8.0 %shard_map.64 = bf16[4,256,512]{2,1,0:T(8,128)(2,1)} custom-call(s32[2]{0:T(128)} %pad_add_fusion.place_ref, f32[1,8]{1,0:T(1,128)} %scale_ref.1, f32[256,256]{1,0:T(8,128)} %right_ref.1, bf16[2048,256]{1,0:T(8,128)(2,1)} %prior_ref.1, bf16[2048,2048]{1,0:T(8,128)(2,1)} %codes_ref.1), custom_call_target="tpu_custom_call" | custom-call | flops 2147483648 | bytes 10485760 | tf_op jit(solution)/shard_map/pallas_call | solution.py:238
  8.6 7.6 %all-to-all-start = ((bf16[16,64,512]{2,1,0:T(8,128)(2,1)}), bf16[16,64,512]{2,1,0:T(8,128)(2,1)}, u32[]{:S(2)}, u32[]{:S(2)}) async-start(bf16[16,64,512]{2,1,0:T(8,128)(2,1)} %bitcast.58), calls=%async_computation | async-start | bytes 2097152 | tf_op jit(solution)/shard_map/all_to_all | solution.py:331
  16.3 1.9 %collective-permute-start.4 = (bf16[256,2048]{1,0:T(8,128)(2,1)S(1)}, bf16[256,2048]{1,0:T(8,128)(2,1)}, u32[]{:S(2)}, u32[]{:S(2)}) collective-permute-start(bf16[256,2048]{1,0:T(8,128)(2,1)S(1)} %bitcast.59), channel_id=1, source_target_pairs={{0,4},{1,5},{2,6},{3,7},{4,0},{5,1},{6,2},{7,3},{8,12},{9,13},{10,... | collective-permute-start | bytes 3145736 | tf_op jit(solution)/shard_map/ppermute | solution.py:29
  18.2 2.3 %dynamic-slice_bitcast_fusion = bf16[256,2048]{1,0:T(8,128)(2,1)} fusion(bf16[1,4,256,2048]{3,2,1,0:T(8,128)(2,1)} %param.11, s32[]{:T(128)S(6)} %select_n.229), kind=kLoop, calls=%fused_computation.2 | loop fusion | bytes 2097156 | tf_op jit(solution)/shard_map/jit(dynamic_index_in_dim)/squeeze | solution.py:312
  20.5 1.7 collective-permute-start.14
  22.2 0.8 collective-permute-start.13
  23.0 1.8 %slice_bitcast_fusion.own_ref = bf16[2,256,2048]{2,1,0:T(8,128)(2,1)S(1)} fusion(bf16[1,4,256,2048]{3,2,1,0:T(8,128)(2,1)} %param.11), kind=kLoop, calls=%fused_computation.1 | loop fusion | bytes 4194304 | tf_op jit(solution)/shard_map/squeeze | solution.py:310
  24.8 2.0 %collective-permute-start.10 = (bf16[2,256,2048]{2,1,0:T(8,128)(2,1)S(1)}, bf16[2,256,2048]{2,1,0:T(8,128)(2,1)}, u32[]{:S(2)}, u32[]{:S(2)}) collective-permute-start(bf16[2,256,2048]{2,1,0:T(8,128)(2,1)S(1)} %slice_bitcast_fusion.own_ref), channel_id=1, source_target_pairs={{2,6},{3,7},{6,2},{7,3},{10,14},{11,15},{14,10},{15,11},{18,22},{1... | collective-permute-start | bytes 6291464 | tf_op jit(solution)/shard_map/ppermute | solution.py:29
  26.8 26.8 %collective-permute-done.4 = bf16[256,2048]{1,0:T(8,128)(2,1)} collective-permute-done((bf16[256,2048]{1,0:T(8,128)(2,1)S(1)}, bf16[256,2048]{1,0:T(8,128)(2,1)}, u32[]{:S(2)}, u32[]{:S(2)}) %collective-permute-start.4) | collective-permute-done | bytes 1048608 | tf_op jit(solution)/shard_map/ppermute | solution.py:29
  54.2 2.7 %broadcast_select_fusion.2 = (bf16[256,2048]{1,0:T(8,128)(2,1)S(1)}, bf16[256,2048]{1,0:T(8,128)(2,1)}) fusion(bf16[256,2048]{1,0:T(8,128)(2,1)} %collective-permute-done.3, pred[]{:T(512)S(6)} %eq.7, bf16[1,256,2048]{2,1,0:T(8,128)(2,1)} %param.10), kind=kLoop, calls=%fused_computation.5 | loop fusion | flops 1048576 | bytes 4194305 | tf_op jit(solution)/shard_map/jit(_where)/select_n | solution.py:300
  56.9 1.4 convert_reduce_fusion
  58.4 1.5 collective-permute-start
  59.9 1.7 broadcast_select_fusion.4
  61.6 2.7 %collective-permute-start.15 = (bf16[256,2048]{1,0:T(8,128)(2,1)}, bf16[256,2048]{1,0:T(8,128)(2,1)S(1)}, u32[]{:S(2)}, u32[]{:S(2)}) collective-permute-start(bf16[256,2048]{1,0:T(8,128)(2,1)} %collective-permute-done.14), channel_id=1, source_target_pairs={{0,1},{1,0},{2,3},{3,2},{4,5},{5,4},{6,7},{7,6},{8,9},{9,8},{10,11... | collective-permute-start | bytes 3145736 | tf_op jit(solution)/shard_map/ppermute | solution.py:29
  64.5 2.0 %collective-permute-start.1 = (bf16[64,512]{1,0:T(8,128)(2,1)S(1)}, bf16[64,512]{1,0:T(8,128)(2,1)S(1)}, u32[]{:S(2)}, u32[]{:S(2)}) collective-permute-start(bf16[64,512]{1,0:T(8,128)(2,1)S(1)} %get-tuple-element.23), channel_id=1, source_target_pairs={{0,16},{1,17},{2,18},{3,19},{4,20},{5,21},{6,22},{7,23},{8,24},{9,... | collective-permute-start | bytes 196616 | tf_op jit(solution)/shard_map/ppermute | solution.py:29
  66.5 4.1 %collective-permute-done.1 = bf16[64,512]{1,0:T(8,128)(2,1)S(1)} collective-permute-done((bf16[64,512]{1,0:T(8,128)(2,1)S(1)}, bf16[64,512]{1,0:T(8,128)(2,1)S(1)}, u32[]{:S(2)}, u32[]{:S(2)}) %collective-permute-start.1) | collective-permute-done | bytes 65568 | tf_op jit(solution)/shard_map/ppermute | solution.py:29
  70.7 3.1 %collective-permute-start.2 = (bf16[64,512]{1,0:T(8,128)(2,1)S(1)}, bf16[64,512]{1,0:T(8,128)(2,1)S(1)}, u32[]{:S(2)}, u32[]{:S(2)}) collective-permute-start(bf16[64,512]{1,0:T(8,128)(2,1)S(1)} %get-tuple-element.23), channel_id=1, source_target_pairs={{0,24},{1,25},{2,26},{3,27},{4,28},{5,29},{6,30},{7,31},{8,0},{9,1... | collective-permute-start | bytes 196616 | tf_op jit(solution)/shard_map/ppermute | solution.py:29
  73.7 1.9 %collective-permute-done.2 = bf16[64,512]{1,0:T(8,128)(2,1)S(1)} collective-permute-done((bf16[64,512]{1,0:T(8,128)(2,1)S(1)}, bf16[64,512]{1,0:T(8,128)(2,1)S(1)}, u32[]{:S(2)}, u32[]{:S(2)}) %collective-permute-start.2) | collective-permute-done | bytes 65568 | tf_op jit(solution)/shard_map/ppermute | solution.py:29
  75.7 2.7 %broadcast_select_fusion.1 = (bf16[256,2048]{1,0:T(8,128)(2,1)}, bf16[256,2048]{1,0:T(8,128)(2,1)S(1)}) fusion(bf16[256,2048]{1,0:T(8,128)(2,1)} %collective-permute-done.5, bf16[256,2048]{1,0:T(8,128)(2,1)} %collective-permute-done.4, pred[]{:T(512)S(6)} %eq.7), kind=kLoop, calls=%fused_computation.4 | loop fusion | flops 1048576 | bytes 4194305 | tf_op jit(solution)/shard_map/jit(_where)/select_n | solution.py:300
  79.4 4.7 %collective-permute-start.7 = (bf16[64,512]{1,0:T(8,128)(2,1)S(1)}, bf16[64,512]{1,0:T(8,128)(2,1)S(1)}, u32[]{:S(2)}, u32[]{:S(2)}) collective-permute-start(bf16[64,512]{1,0:T(8,128)(2,1)S(1)} %get-tuple-element.46), channel_id=1, source_target_pairs={{0,16},{1,17},{2,18},{3,19},{4,20},{5,21},{6,22},{7,23},{8,24},{9,... | collective-permute-start | bytes 196616 | tf_op jit(solution)/shard_map/ppermute | solution.py:29
  84.4 1.7 collective-permute-done.6
  86.1 2.0 %collective-permute-done.7 = bf16[64,512]{1,0:T(8,128)(2,1)S(1)} collective-permute-done((bf16[64,512]{1,0:T(8,128)(2,1)S(1)}, bf16[64,512]{1,0:T(8,128)(2,1)S(1)}, u32[]{:S(2)}, u32[]{:S(2)}) %collective-permute-start.7) | collective-permute-done | bytes 65568 | tf_op jit(solution)/shard_map/ppermute | solution.py:29
  89.6 0.7 broadcast.6.clone.2
  90.3 0.7 constant_dynamic-update-slice_fusion.19
  90.9 0.7 collective-permute-start.16
  91.6 1.7 collective-permute-start.29
  93.3 2.2 %collective-permute-start.17 = (bf16[64,512]{1,0:T(8,128)(2,1)S(1)}, bf16[64,512]{1,0:T(8,128)(2,1)S(1)}, u32[]{:S(2)}, u32[]{:S(2)}) collective-permute-start(bf16[64,512]{1,0:T(8,128)(2,1)S(1)} %get-tuple-element.21), channel_id=1, source_target_pairs={{0,16},{1,17},{2,18},{3,19},{4,20},{5,21},{6,22},{7,23},{8,24},{9,... | collective-permute-start | bytes 196616 | tf_op jit(solution)/shard_map/ppermute | solution.py:29
  95.5 1.9 %collective-permute-done.16 = bf16[64,512]{1,0:T(8,128)(2,1)S(1)} collective-permute-done((bf16[64,512]{1,0:T(8,128)(2,1)S(1)}, bf16[64,512]{1,0:T(8,128)(2,1)S(1)}, u32[]{:S(2)}, u32[]{:S(2)}) %collective-permute-start.16) | collective-permute-done | bytes 65568 | tf_op jit(solution)/shard_map/ppermute | solution.py:29
  97.5 0.6 constant_dynamic-update-slice_fusion.18
  98.1 1.3 collective-permute-done.17
  99.4 0.6 constant_dynamic-update-slice_fusion.17
  100.0 1.6 collective-permute-done.18
  101.7 0.6 constant_dynamic-update-slice_fusion.16
  102.3 1.8 fusion.11
  104.1 1.4 broadcast_select_fusion.28
  105.5 11.4 %collective-permute-start.19 = (bf16[64,512]{1,0:T(8,128)(2,1)S(1)}, bf16[64,512]{1,0:T(8,128)(2,1)S(1)}, u32[]{:S(2)}, u32[]{:S(2)}) collective-permute-start(bf16[64,512]{1,0:T(8,128)(2,1)S(1)} %fusion.3), channel_id=1, source_target_pairs={{0,2},{1,3},{2,0},{3,1},{4,6},{5,7},{6,4},{7,5},{8,10},{9,11},{10,... | collective-permute-start | bytes 196616 | tf_op jit(solution)/shard_map/ppermute | solution.py:29
  116.9 2.5 %collective-permute-start.9 = (bf16[64,2048]{1,0:T(8,128)(2,1)S(1)}, bf16[64,2048]{1,0:T(8,128)(2,1)S(1)}, u32[]{:S(2)}, u32[]{:S(2)}) collective-permute-start(bf16[64,2048]{1,0:T(8,128)(2,1)S(1)} %constant_dynamic-update-slice_fusion.20), channel_id=1, source_target_pairs={{0,2},{1,3},{2,0},{3,1},{4,6},{5,7},{6,4},{7,5},{8,10},{9,11},{10,... | collective-permute-start | bytes 786440 | tf_op jit(solution)/shard_map/ppermute | solution.py:29
  119.4 1.5 collective-permute-start.20
  121.0 4.6 %collective-permute-done.20 = bf16[64,512]{1,0:T(8,128)(2,1)S(1)} collective-permute-done((bf16[64,512]{1,0:T(8,128)(2,1)S(1)}, bf16[64,512]{1,0:T(8,128)(2,1)S(1)}, u32[]{:S(2)}, u32[]{:S(2)}) %collective-permute-start.20) | collective-permute-done | bytes 65568 | tf_op jit(solution)/shard_map/ppermute | solution.py:29
  125.5 0.8 collective-permute-start.21
  126.3 5.0 %collective-permute-done.21 = bf16[64,512]{1,0:T(8,128)(2,1)S(1)} collective-permute-done((bf16[64,512]{1,0:T(8,128)(2,1)S(1)}, bf16[64,512]{1,0:T(8,128)(2,1)S(1)}, u32[]{:S(2)}, u32[]{:S(2)}) %collective-permute-start.21) | collective-permute-done | bytes 65568 | tf_op jit(solution)/shard_map/ppermute | solution.py:29
  131.3 4.2 %collective-permute-done.22 = bf16[64,512]{1,0:T(8,128)(2,1)S(1)} collective-permute-done((bf16[64,512]{1,0:T(8,128)(2,1)S(1)}, bf16[64,512]{1,0:T(8,128)(2,1)S(1)}, u32[]{:S(2)}, u32[]{:S(2)}) %collective-permute-start.22) | collective-permute-done | bytes 65568 | tf_op jit(solution)/shard_map/ppermute | solution.py:29
  135.5 2.6 %shard_map.66 = f32[64,512]{1,0:T(8,128)S(1)} custom-call(s32[2]{0:T(128)S(1)} %pad_add_fusion.1.flags, bf16[64,2048]{1,0:T(8,128)(2,1)S(1)} %constant_dynamic-update-slice_fusion.12.vector_ref, bf16[2,256,2048]{2,1,0:T(8,128)(2,1)S(1)} %slice_bitcast_fusion.own_ref, bf16[2,256,2048]{2,1,0:T(8,128)(2,1)} %collective-permute-done.10.own_y_ref, ...), custom_call_target="tpu_custom_call" | custom-call | flops 134217728 | bytes 2097152 | tf_op jit(solution)/shard_map/pallas_call | solution.py:194
  138.2 2.6 %shard_map.65 = f32[64,512]{1,0:T(8,128)S(1)} custom-call(s32[2]{0:T(128)S(1)} %pad_add_fusion.1.flags, bf16[64,2048]{1,0:T(8,128)(2,1)S(1)} %collective-permute-done.9.vector_ref, bf16[2,256,2048]{2,1,0:T(8,128)(2,1)S(1)} %slice_bitcast_fusion.own_ref, bf16[2,256,2048]{2,1,0:T(8,128)(2,1)} %collective-permute-done.10.own_y_ref, ...), custom_call_target="tpu_custom_call" | custom-call | flops 134217728 | bytes 2097152 | tf_op jit(solution)/shard_map/pallas_call | solution.py:194
  141.0 2.4 %collective-permute-start.24 = (bf16[64,512]{1,0:T(8,128)(2,1)S(1)}, bf16[64,512]{1,0:T(8,128)(2,1)S(1)}, u32[]{:S(2)}, u32[]{:S(2)}) collective-permute-start(bf16[64,512]{1,0:T(8,128)(2,1)S(1)} %get-tuple-element.19), channel_id=1, source_target_pairs={{0,16},{1,17},{2,18},{3,19},{4,20},{5,21},{6,22},{7,23},{8,24},{9,... | collective-permute-start | bytes 196616 | tf_op jit(solution)/shard_map/ppermute | solution.py:29
  143.4 1.5 collective-permute-start.25
  144.9 2.1 %collective-permute-done.23 = bf16[64,512]{1,0:T(8,128)(2,1)S(1)} collective-permute-done((bf16[64,512]{1,0:T(8,128)(2,1)S(1)}, bf16[64,512]{1,0:T(8,128)(2,1)S(1)}, u32[]{:S(2)}, u32[]{:S(2)}) %collective-permute-start.23) | collective-permute-done | bytes 65568 | tf_op jit(solution)/shard_map/ppermute | solution.py:29
  147.0 0.7 collective-permute-done.25
  148.6 2.0 %collective-permute-start.26 = (bf16[64,512]{1,0:T(8,128)(2,1)S(1)}, bf16[64,512]{1,0:T(8,128)(2,1)S(1)}, u32[]{:S(2)}, u32[]{:S(2)}) collective-permute-start(bf16[64,512]{1,0:T(8,128)(2,1)S(1)} %get-tuple-element.44), channel_id=1, source_target_pairs={{0,8},{1,9},{2,10},{3,11},{4,12},{5,13},{6,14},{7,15},{8,16},{9,17... | collective-permute-start | bytes 196616 | tf_op jit(solution)/shard_map/ppermute | solution.py:29
  150.8 3.2 %shard_map.68 = f32[64,512]{1,0:T(8,128)S(1)} custom-call(s32[2]{0:T(128)S(1)} %pad_add_fusion.2.flags, bf16[64,2048]{1,0:T(8,128)(2,1)S(1)} %constant_dynamic-update-slice_fusion.12.vector_ref, bf16[2,256,2048]{2,1,0:T(8,128)(2,1)S(1)} %slice_bitcast_fusion.own_ref, bf16[2,256,2048]{2,1,0:T(8,128)(2,1)} %collective-permute-done.10.own_y_ref, ...), custom_call_target="tpu_custom_call" | custom-call | flops 134217728 | bytes 2097152 | tf_op jit(solution)/shard_map/pallas_call | solution.py:194
  154.0 3.2 %shard_map.67 = f32[64,512]{1,0:T(8,128)S(1)} custom-call(s32[2]{0:T(128)S(1)} %pad_add_fusion.2.flags, bf16[64,2048]{1,0:T(8,128)(2,1)S(1)} %collective-permute-done.9.vector_ref, bf16[2,256,2048]{2,1,0:T(8,128)(2,1)S(1)} %slice_bitcast_fusion.own_ref, bf16[2,256,2048]{2,1,0:T(8,128)(2,1)} %collective-permute-done.10.own_y_ref, ...), custom_call_target="tpu_custom_call" | custom-call | flops 134217728 | bytes 2097152 | tf_op jit(solution)/shard_map/pallas_call | solution.py:194
  157.3 2.1 %collective-permute-start.27 = (bf16[64,512]{1,0:T(8,128)(2,1)S(1)}, bf16[64,512]{1,0:T(8,128)(2,1)S(1)}, u32[]{:S(2)}, u32[]{:S(2)}) collective-permute-start(bf16[64,512]{1,0:T(8,128)(2,1)S(1)} %get-tuple-element.44), channel_id=1, source_target_pairs={{0,16},{1,17},{2,18},{3,19},{4,20},{5,21},{6,22},{7,23},{8,24},{9,... | collective-permute-start | bytes 196616 | tf_op jit(solution)/shard_map/ppermute | solution.py:29
  159.8 2.9 %collective-permute-done.27 = bf16[64,512]{1,0:T(8,128)(2,1)S(1)} collective-permute-done((bf16[64,512]{1,0:T(8,128)(2,1)S(1)}, bf16[64,512]{1,0:T(8,128)(2,1)S(1)}, u32[]{:S(2)}, u32[]{:S(2)}) %collective-permute-start.27) | collective-permute-done | bytes 65568 | tf_op jit(solution)/shard_map/ppermute | solution.py:29
  162.7 0.9 collective-permute-done.28
  165.1 3.1 %collective-permute-start.32 = (bf16[64,512]{1,0:T(8,128)(2,1)S(1)}, bf16[64,512]{1,0:T(8,128)(2,1)S(1)}, u32[]{:S(2)}, u32[]{:S(2)}) collective-permute-start(bf16[64,512]{1,0:T(8,128)(2,1)S(1)} %get-tuple-element.13), channel_id=1, source_target_pairs={{0,16},{1,17},{2,18},{3,19},{4,20},{5,21},{6,22},{7,23},{8,24},{9,... | collective-permute-start | bytes 196616 | tf_op jit(solution)/shard_map/ppermute | solution.py:29
  168.2 0.8 collective-permute-start.33
  169.0 1.9 %collective-permute-done.31 = bf16[64,512]{1,0:T(8,128)(2,1)S(1)} collective-permute-done((bf16[64,512]{1,0:T(8,128)(2,1)S(1)}, bf16[64,512]{1,0:T(8,128)(2,1)S(1)}, u32[]{:S(2)}, u32[]{:S(2)}) %collective-permute-start.31) | collective-permute-done | bytes 65568 | tf_op jit(solution)/shard_map/ppermute | solution.py:29
  170.9 1.0 collective-permute-done.32
  171.9 0.7 collective-permute-done.33
  173.6 2.8 %collective-permute-start.35 = (f32[64,256]{1,0:T(8,128)S(1)}, f32[64,256]{1,0:T(8,128)S(1)}, u32[]{:S(2)}, u32[]{:S(2)}) collective-permute-start(f32[64,256]{1,0:T(8,128)S(1)} %get-tuple-element.30), channel_id=1, source_target_pairs={{0,4},{1,5},{2,6},{3,7},{4,0},{5,1},{6,2},{7,3},{8,12},{9,13},{10,... | collective-permute-start | bytes 196616 | tf_op jit(solution)/shard_map/ppermute | solution.py:29
  176.4 2.6 %collective-permute-done.35 = f32[64,256]{1,0:T(8,128)S(1)} collective-permute-done((f32[64,256]{1,0:T(8,128)S(1)}, f32[64,256]{1,0:T(8,128)S(1)}, u32[]{:S(2)}, u32[]{:S(2)}) %collective-permute-start.35) | collective-permute-done | bytes 65568 | tf_op jit(solution)/shard_map/ppermute | solution.py:29
  179.1 1.4 collective-permute-done.36
  180.5 0.8 copy.7
  (102 shorter events, 7.9 us)
Async XLA Ops:
  8.6 7.6 %copy-start.9 = (bf16[1,256,2048]{2,1,0:T(8,128)(2,1)S(1)}, bf16[1,256,2048]{2,1,0:T(8,128)(2,1)}, u32[]{:S(2)}) copy-start(bf16[1,256,2048]{2,1,0:T(8,128)(2,1)} %param.10) | copy-start | bytes 3145732
  8.6 48.3 %all-to-all-start = ((bf16[16,64,512]{2,1,0:T(8,128)(2,1)}), bf16[16,64,512]{2,1,0:T(8,128)(2,1)}, u32[]{:S(2)}, u32[]{:S(2)}) async-start(bf16[16,64,512]{2,1,0:T(8,128)(2,1)} %bitcast.58), calls=%async_computation | async-start | bytes 2097152 | tf_op jit(solution)/shard_map/all_to_all | solution.py:331
  16.3 37.4 %collective-permute-start.4 = (bf16[256,2048]{1,0:T(8,128)(2,1)S(1)}, bf16[256,2048]{1,0:T(8,128)(2,1)}, u32[]{:S(2)}, u32[]{:S(2)}) collective-permute-start(bf16[256,2048]{1,0:T(8,128)(2,1)S(1)} %bitcast.59), channel_id=1, source_target_pairs={{0,4},{1,5},{2,6},{3,7},{4,0},{5,1},{6,2},{7,3},{8,12},{9,13},{10,... | collective-permute-start | bytes 3145736 | tf_op jit(solution)/shard_map/ppermute | solution.py:29
  18.2 35.5 %collective-permute-start.3 = (bf16[256,2048]{1,0:T(8,128)(2,1)S(1)}, bf16[256,2048]{1,0:T(8,128)(2,1)}, u32[]{:S(2)}, u32[]{:S(2)}) collective-permute-start(bf16[256,2048]{1,0:T(8,128)(2,1)S(1)} %bitcast.60), channel_id=1, source_target_pairs={{0,1},{1,0},{2,3},{3,2},{4,5},{5,4},{6,7},{7,6},{8,9},{9,8},{10,11... | collective-permute-start | bytes 3145736 | tf_op jit(solution)/shard_map/ppermute | solution.py:29
  20.5 41.1 %collective-permute-start.14 = (bf16[256,2048]{1,0:T(8,128)(2,1)}, bf16[256,2048]{1,0:T(8,128)(2,1)}, u32[]{:S(2)}, u32[]{:S(2)}) collective-permute-start(bf16[256,2048]{1,0:T(8,128)(2,1)} %dynamic-slice_bitcast_fusion), channel_id=1, source_target_pairs={{1,5},{5,1},{9,13},{13,9},{17,21},{21,17},{25,29},{29,25}} | collective-permute-start | bytes 3145736 | tf_op jit(solution)/shard_map/ppermute | solution.py:29
  22.2 36.2 %collective-permute-start.13 = (bf16[256,2048]{1,0:T(8,128)(2,1)}, bf16[256,2048]{1,0:T(8,128)(2,1)}, u32[]{:S(2)}, u32[]{:S(2)}) collective-permute-start(bf16[256,2048]{1,0:T(8,128)(2,1)} %dynamic-slice_bitcast_fusion), channel_id=1, source_target_pairs={{0,1},{1,0},{2,3},{3,2},{4,5},{5,4},{6,7},{7,6},{8,9},{9,8},{10,11... | collective-permute-start | bytes 3145736 | tf_op jit(solution)/shard_map/ppermute | solution.py:29
  24.8 59.5 %collective-permute-start.10 = (bf16[2,256,2048]{2,1,0:T(8,128)(2,1)S(1)}, bf16[2,256,2048]{2,1,0:T(8,128)(2,1)}, u32[]{:S(2)}, u32[]{:S(2)}) collective-permute-start(bf16[2,256,2048]{2,1,0:T(8,128)(2,1)S(1)} %slice_bitcast_fusion.own_ref), channel_id=1, source_target_pairs={{2,6},{3,7},{6,2},{7,3},{10,14},{11,15},{14,10},{15,11},{18,22},{1... | collective-permute-start | bytes 6291464 | tf_op jit(solution)/shard_map/ppermute | solution.py:29
  53.7 81.9 %collective-permute-start.11 = (bf16[2,256,2048]{2,1,0:T(8,128)(2,1)S(1)}, bf16[2,256,2048]{2,1,0:T(8,128)(2,1)}, u32[]{:S(2)}, u32[]{:S(2)}) collective-permute-start(bf16[2,256,2048]{2,1,0:T(8,128)(2,1)S(1)} %slice_bitcast_fusion.own_ref), channel_id=1, source_target_pairs={{0,1},{1,0},{2,3},{3,2},{4,5},{5,4},{6,7},{7,6},{8,9},{9,8},{10,11... | collective-permute-start | bytes 6291464 | tf_op jit(solution)/shard_map/ppermute | solution.py:29
  53.7 22.0 %collective-permute-start.5 = (bf16[256,2048]{1,0:T(8,128)(2,1)}, bf16[256,2048]{1,0:T(8,128)(2,1)}, u32[]{:S(2)}, u32[]{:S(2)}) collective-permute-start(bf16[256,2048]{1,0:T(8,128)(2,1)} %collective-permute-done.4), channel_id=1, source_target_pairs={{0,1},{1,0},{2,3},{3,2},{4,5},{5,4},{6,7},{7,6},{8,9},{9,8},{10,11... | collective-permute-start | bytes 3145736 | tf_op jit(solution)/shard_map/ppermute | solution.py:29
  58.3 32.0 %copy-start.7 = (f32[2,64,512]{2,1,0:T(8,128)}, f32[2,64,512]{2,1,0:T(8,128)S(1)}, u32[]{:S(2)}) copy-start(f32[2,64,512]{2,1,0:T(8,128)S(1)} %convert_reduce_fusion) | copy-start | bytes 786436
  58.4 6.1 %collective-permute-start = (bf16[64,512]{1,0:T(8,128)(2,1)S(1)}, bf16[64,512]{1,0:T(8,128)(2,1)S(1)}, u32[]{:S(2)}, u32[]{:S(2)}) collective-permute-start(bf16[64,512]{1,0:T(8,128)(2,1)S(1)} %get-tuple-element.23), channel_id=1, source_target_pairs={{0,8},{1,9},{2,10},{3,11},{4,12},{5,13},{6,14},{7,15},{8,16},{9,17... | collective-permute-start | bytes 196616 | tf_op jit(solution)/shard_map/ppermute | solution.py:29
  61.6 27.5 %copy-start.5 = (bf16[256,2048]{1,0:T(8,128)(2,1)}, bf16[256,2048]{1,0:T(8,128)(2,1)S(1)}, u32[]{:S(2)}) copy-start(bf16[256,2048]{1,0:T(8,128)(2,1)S(1)} %broadcast_select_fusion.4) | copy-start | bytes 3145732
  61.6 22.5 %collective-permute-start.15 = (bf16[256,2048]{1,0:T(8,128)(2,1)}, bf16[256,2048]{1,0:T(8,128)(2,1)S(1)}, u32[]{:S(2)}, u32[]{:S(2)}) collective-permute-start(bf16[256,2048]{1,0:T(8,128)(2,1)} %collective-permute-done.14), channel_id=1, source_target_pairs={{0,1},{1,0},{2,3},{3,2},{4,5},{5,4},{6,7},{7,6},{8,9},{9,8},{10,11... | collective-permute-start | bytes 3145736 | tf_op jit(solution)/shard_map/ppermute | solution.py:29
  64.5 6.1 %collective-permute-start.1 = (bf16[64,512]{1,0:T(8,128)(2,1)S(1)}, bf16[64,512]{1,0:T(8,128)(2,1)S(1)}, u32[]{:S(2)}, u32[]{:S(2)}) collective-permute-start(bf16[64,512]{1,0:T(8,128)(2,1)S(1)} %get-tuple-element.23), channel_id=1, source_target_pairs={{0,16},{1,17},{2,18},{3,19},{4,20},{5,21},{6,22},{7,23},{8,24},{9,... | collective-permute-start | bytes 196616 | tf_op jit(solution)/shard_map/ppermute | solution.py:29
  70.7 5.0 %collective-permute-start.2 = (bf16[64,512]{1,0:T(8,128)(2,1)S(1)}, bf16[64,512]{1,0:T(8,128)(2,1)S(1)}, u32[]{:S(2)}, u32[]{:S(2)}) collective-permute-start(bf16[64,512]{1,0:T(8,128)(2,1)S(1)} %get-tuple-element.23), channel_id=1, source_target_pairs={{0,24},{1,25},{2,26},{3,27},{4,28},{5,29},{6,30},{7,31},{8,0},{9,1... | collective-permute-start | bytes 196616 | tf_op jit(solution)/shard_map/ppermute | solution.py:29
  75.6 3.2 %copy-start.1 = (bf16[256,2048]{1,0:T(8,128)(2,1)S(1)}, bf16[256,2048]{1,0:T(8,128)(2,1)}, u32[]{:S(2)}) copy-start(bf16[256,2048]{1,0:T(8,128)(2,1)} %get-tuple-element.25) | copy-start | bytes 3145732
  78.4 5.9 %copy-start.3 = (bf16[256,2048]{1,0:T(8,128)(2,1)}, bf16[256,2048]{1,0:T(8,128)(2,1)S(1)}, u32[]{:S(2)}) copy-start(bf16[256,2048]{1,0:T(8,128)(2,1)S(1)} %get-tuple-element.27) | copy-start | bytes 3145732
  79.4 6.7 %collective-permute-start.6 = (bf16[64,512]{1,0:T(8,128)(2,1)S(1)}, bf16[64,512]{1,0:T(8,128)(2,1)S(1)}, u32[]{:S(2)}, u32[]{:S(2)}) collective-permute-start(bf16[64,512]{1,0:T(8,128)(2,1)S(1)} %get-tuple-element.46), channel_id=1, source_target_pairs={{0,8},{1,9},{2,10},{3,11},{4,12},{5,13},{6,14},{7,15},{8,16},{9,17... | collective-permute-start | bytes 196616 | tf_op jit(solution)/shard_map/ppermute | solution.py:29
  79.4 8.7 %collective-permute-start.7 = (bf16[64,512]{1,0:T(8,128)(2,1)S(1)}, bf16[64,512]{1,0:T(8,128)(2,1)S(1)}, u32[]{:S(2)}, u32[]{:S(2)}) collective-permute-start(bf16[64,512]{1,0:T(8,128)(2,1)S(1)} %get-tuple-element.46), channel_id=1, source_target_pairs={{0,16},{1,17},{2,18},{3,19},{4,20},{5,21},{6,22},{7,23},{8,24},{9,... | collective-permute-start | bytes 196616 | tf_op jit(solution)/shard_map/ppermute | solution.py:29
  84.1 4.5 %collective-permute-start.8 = (bf16[64,512]{1,0:T(8,128)(2,1)S(1)}, bf16[64,512]{1,0:T(8,128)(2,1)S(1)}, u32[]{:S(2)}, u32[]{:S(2)}) collective-permute-start(bf16[64,512]{1,0:T(8,128)(2,1)S(1)} %get-tuple-element.46), channel_id=1, source_target_pairs={{0,24},{1,25},{2,26},{3,27},{4,28},{5,29},{6,30},{7,31},{8,0},{9,1... | collective-permute-start | bytes 196616 | tf_op jit(solution)/shard_map/ppermute | solution.py:29
  84.3 51.2 %collective-permute-start.12 = (bf16[2,256,2048]{2,1,0:T(8,128)(2,1)}, bf16[2,256,2048]{2,1,0:T(8,128)(2,1)}, u32[]{:S(2)}, u32[]{:S(2)}) collective-permute-start(bf16[2,256,2048]{2,1,0:T(8,128)(2,1)} %collective-permute-done.10.own_y_ref), channel_id=1, source_target_pairs={{0,1},{1,0},{2,3},{3,2},{4,5},{5,4},{6,7},{7,6},{8,9},{9,8},{10,11... | collective-permute-start | bytes 6291464 | tf_op jit(solution)/shard_map/ppermute | solution.py:29
  90.9 6.5 %collective-permute-start.16 = (bf16[64,512]{1,0:T(8,128)(2,1)S(1)}, bf16[64,512]{1,0:T(8,128)(2,1)S(1)}, u32[]{:S(2)}, u32[]{:S(2)}) collective-permute-start(bf16[64,512]{1,0:T(8,128)(2,1)S(1)} %get-tuple-element.21), channel_id=1, source_target_pairs={{0,8},{1,9},{2,10},{3,11},{4,12},{5,13},{6,14},{7,15},{8,16},{9,17... | collective-permute-start | bytes 196616 | tf_op jit(solution)/shard_map/ppermute | solution.py:29
  91.6 25.3 %collective-permute-start.29 = (bf16[256,2048]{1,0:T(8,128)(2,1)}, bf16[256,2048]{1,0:T(8,128)(2,1)}, u32[]{:S(2)}, u32[]{:S(2)}) collective-permute-start(bf16[256,2048]{1,0:T(8,128)(2,1)} %dynamic-slice_bitcast_fusion), channel_id=1, source_target_pairs={{3,7},{7,3},{11,15},{15,11},{19,23},{23,19},{27,31},{31,27}} | collective-permute-start | bytes 3145736 | tf_op jit(solution)/shard_map/ppermute | solution.py:29
  93.3 6.1 %collective-permute-start.17 = (bf16[64,512]{1,0:T(8,128)(2,1)S(1)}, bf16[64,512]{1,0:T(8,128)(2,1)S(1)}, u32[]{:S(2)}, u32[]{:S(2)}) collective-permute-start(bf16[64,512]{1,0:T(8,128)(2,1)S(1)} %get-tuple-element.21), channel_id=1, source_target_pairs={{0,16},{1,17},{2,18},{3,19},{4,20},{5,21},{6,22},{7,23},{8,24},{9,... | collective-permute-start | bytes 196616 | tf_op jit(solution)/shard_map/ppermute | solution.py:29
  97.4 4.3 %collective-permute-start.18 = (bf16[64,512]{1,0:T(8,128)(2,1)S(1)}, bf16[64,512]{1,0:T(8,128)(2,1)S(1)}, u32[]{:S(2)}, u32[]{:S(2)}) collective-permute-start(bf16[64,512]{1,0:T(8,128)(2,1)S(1)} %get-tuple-element.21), channel_id=1, source_target_pairs={{0,24},{1,25},{2,26},{3,27},{4,28},{5,29},{6,30},{7,31},{8,0},{9,1... | collective-permute-start | bytes 196616 | tf_op jit(solution)/shard_map/ppermute | solution.py:29
  105.5 14.0 %collective-permute-start.19 = (bf16[64,512]{1,0:T(8,128)(2,1)S(1)}, bf16[64,512]{1,0:T(8,128)(2,1)S(1)}, u32[]{:S(2)}, u32[]{:S(2)}) collective-permute-start(bf16[64,512]{1,0:T(8,128)(2,1)S(1)} %fusion.3), channel_id=1, source_target_pairs={{0,2},{1,3},{2,0},{3,1},{4,6},{5,7},{6,4},{7,5},{8,10},{9,11},{10,... | collective-permute-start | bytes 196616 | tf_op jit(solution)/shard_map/ppermute | solution.py:29
  116.9 33.7 %collective-permute-start.30 = (bf16[256,2048]{1,0:T(8,128)(2,1)}, bf16[256,2048]{1,0:T(8,128)(2,1)S(1)}, u32[]{:S(2)}, u32[]{:S(2)}) collective-permute-start(bf16[256,2048]{1,0:T(8,128)(2,1)} %collective-permute-done.29), channel_id=1, source_target_pairs={{0,1},{1,0},{2,3},{3,2},{4,5},{5,4},{6,7},{7,6},{8,9},{9,8},{10,11... | collective-permute-start | bytes 3145736 | tf_op jit(solution)/shard_map/ppermute | solution.py:29
  116.9 21.2 %collective-permute-start.9 = (bf16[64,2048]{1,0:T(8,128)(2,1)S(1)}, bf16[64,2048]{1,0:T(8,128)(2,1)S(1)}, u32[]{:S(2)}, u32[]{:S(2)}) collective-permute-start(bf16[64,2048]{1,0:T(8,128)(2,1)S(1)} %constant_dynamic-update-slice_fusion.20), channel_id=1, source_target_pairs={{0,2},{1,3},{2,0},{3,1},{4,6},{5,7},{6,4},{7,5},{8,10},{9,11},{10,... | collective-permute-start | bytes 786440 | tf_op jit(solution)/shard_map/ppermute | solution.py:29
  119.4 6.1 %collective-permute-start.20 = (bf16[64,512]{1,0:T(8,128)(2,1)S(1)}, bf16[64,512]{1,0:T(8,128)(2,1)S(1)}, u32[]{:S(2)}, u32[]{:S(2)}) collective-permute-start(bf16[64,512]{1,0:T(8,128)(2,1)S(1)} %collective-permute-done.19), channel_id=1, source_target_pairs={{0,8},{1,9},{2,10},{3,11},{4,12},{5,13},{6,14},{7,15},{8,16},{9,17... | collective-permute-start | bytes 196616 | tf_op jit(solution)/shard_map/ppermute | solution.py:29
  125.5 5.7 %collective-permute-start.21 = (bf16[64,512]{1,0:T(8,128)(2,1)S(1)}, bf16[64,512]{1,0:T(8,128)(2,1)S(1)}, u32[]{:S(2)}, u32[]{:S(2)}) collective-permute-start(bf16[64,512]{1,0:T(8,128)(2,1)S(1)} %collective-permute-done.19), channel_id=1, source_target_pairs={{0,16},{1,17},{2,18},{3,19},{4,20},{5,21},{6,22},{7,23},{8,24},{9,... | collective-permute-start | bytes 196616 | tf_op jit(solution)/shard_map/ppermute | solution.py:29
  131.2 4.3 %collective-permute-start.22 = (bf16[64,512]{1,0:T(8,128)(2,1)S(1)}, bf16[64,512]{1,0:T(8,128)(2,1)S(1)}, u32[]{:S(2)}, u32[]{:S(2)}) collective-permute-start(bf16[64,512]{1,0:T(8,128)(2,1)S(1)} %collective-permute-done.19), channel_id=1, source_target_pairs={{0,24},{1,25},{2,26},{3,27},{4,28},{5,29},{6,30},{7,31},{8,0},{9,1... | collective-permute-start | bytes 196616 | tf_op jit(solution)/shard_map/ppermute | solution.py:29
  138.1 2.7 %copy-start.8 = (f32[2,64,512]{2,1,0:T(8,128)S(1)}, f32[2,64,512]{2,1,0:T(8,128)}, u32[]{:S(2)}) copy-start(f32[2,64,512]{2,1,0:T(8,128)} %copy-done.7) | copy-start | bytes 786436
  138.1 9.5 %copy-start.4 = (bf16[256,2048]{1,0:T(8,128)(2,1)S(1)}, bf16[256,2048]{1,0:T(8,128)(2,1)}, u32[]{:S(2)}) copy-start(bf16[256,2048]{1,0:T(8,128)(2,1)} %copy-done.3) | copy-start | bytes 3145732
  140.8 7.4 %copy-start.2 = (bf16[256,2048]{1,0:T(8,128)(2,1)S(1)}, bf16[256,2048]{1,0:T(8,128)(2,1)}, u32[]{:S(2)}) copy-start(bf16[256,2048]{1,0:T(8,128)(2,1)} %get-tuple-element.25) | copy-start | bytes 3145732
  140.8 6.1 %collective-permute-start.23 = (bf16[64,512]{1,0:T(8,128)(2,1)S(1)}, bf16[64,512]{1,0:T(8,128)(2,1)S(1)}, u32[]{:S(2)}, u32[]{:S(2)}) collective-permute-start(bf16[64,512]{1,0:T(8,128)(2,1)S(1)} %get-tuple-element.19), channel_id=1, source_target_pairs={{0,8},{1,9},{2,10},{3,11},{4,12},{5,13},{6,14},{7,15},{8,16},{9,17... | collective-permute-start | bytes 196616 | tf_op jit(solution)/shard_map/ppermute | solution.py:29
  141.0 6.0 %collective-permute-start.24 = (bf16[64,512]{1,0:T(8,128)(2,1)S(1)}, bf16[64,512]{1,0:T(8,128)(2,1)S(1)}, u32[]{:S(2)}, u32[]{:S(2)}) collective-permute-start(bf16[64,512]{1,0:T(8,128)(2,1)S(1)} %get-tuple-element.19), channel_id=1, source_target_pairs={{0,16},{1,17},{2,18},{3,19},{4,20},{5,21},{6,22},{7,23},{8,24},{9,... | collective-permute-start | bytes 196616 | tf_op jit(solution)/shard_map/ppermute | solution.py:29
  143.4 4.3 %collective-permute-start.25 = (bf16[64,512]{1,0:T(8,128)(2,1)S(1)}, bf16[64,512]{1,0:T(8,128)(2,1)S(1)}, u32[]{:S(2)}, u32[]{:S(2)}) collective-permute-start(bf16[64,512]{1,0:T(8,128)(2,1)S(1)} %get-tuple-element.19), channel_id=1, source_target_pairs={{0,24},{1,25},{2,26},{3,27},{4,28},{5,29},{6,30},{7,31},{8,0},{9,1... | collective-permute-start | bytes 196616 | tf_op jit(solution)/shard_map/ppermute | solution.py:29
  148.6 11.1 %collective-permute-start.26 = (bf16[64,512]{1,0:T(8,128)(2,1)S(1)}, bf16[64,512]{1,0:T(8,128)(2,1)S(1)}, u32[]{:S(2)}, u32[]{:S(2)}) collective-permute-start(bf16[64,512]{1,0:T(8,128)(2,1)S(1)} %get-tuple-element.44), channel_id=1, source_target_pairs={{0,8},{1,9},{2,10},{3,11},{4,12},{5,13},{6,14},{7,15},{8,16},{9,17... | collective-permute-start | bytes 196616 | tf_op jit(solution)/shard_map/ppermute | solution.py:29
  154.0 10.1 %copy-start.6 = (bf16[256,2048]{1,0:T(8,128)(2,1)S(1)}, bf16[256,2048]{1,0:T(8,128)(2,1)}, u32[]{:S(2)}) copy-start(bf16[256,2048]{1,0:T(8,128)(2,1)} %copy-done.5) | copy-start | bytes 3145732
  157.3 5.4 %collective-permute-start.27 = (bf16[64,512]{1,0:T(8,128)(2,1)S(1)}, bf16[64,512]{1,0:T(8,128)(2,1)S(1)}, u32[]{:S(2)}, u32[]{:S(2)}) collective-permute-start(bf16[64,512]{1,0:T(8,128)(2,1)S(1)} %get-tuple-element.44), channel_id=1, source_target_pairs={{0,16},{1,17},{2,18},{3,19},{4,20},{5,21},{6,22},{7,23},{8,24},{9,... | collective-permute-start | bytes 196616 | tf_op jit(solution)/shard_map/ppermute | solution.py:29
  159.4 4.3 %collective-permute-start.28 = (bf16[64,512]{1,0:T(8,128)(2,1)S(1)}, bf16[64,512]{1,0:T(8,128)(2,1)S(1)}, u32[]{:S(2)}, u32[]{:S(2)}) collective-permute-start(bf16[64,512]{1,0:T(8,128)(2,1)S(1)} %get-tuple-element.44), channel_id=1, source_target_pairs={{0,24},{1,25},{2,26},{3,27},{4,28},{5,29},{6,30},{7,31},{8,0},{9,1... | collective-permute-start | bytes 196616 | tf_op jit(solution)/shard_map/ppermute | solution.py:29
  163.6 8.9 %copy-start = (bf16[256,2048]{1,0:T(8,128)(2,1)S(1)}, bf16[256,2048]{1,0:T(8,128)(2,1)}, u32[]{:S(2)}) copy-start(bf16[256,2048]{1,0:T(8,128)(2,1)} %get-tuple-element.26) | copy-start | bytes 3145732
  164.6 6.2 %collective-permute-start.31 = (bf16[64,512]{1,0:T(8,128)(2,1)S(1)}, bf16[64,512]{1,0:T(8,128)(2,1)S(1)}, u32[]{:S(2)}, u32[]{:S(2)}) collective-permute-start(bf16[64,512]{1,0:T(8,128)(2,1)S(1)} %get-tuple-element.13), channel_id=1, source_target_pairs={{0,8},{1,9},{2,10},{3,11},{4,12},{5,13},{6,14},{7,15},{8,16},{9,17... | collective-permute-start | bytes 196616 | tf_op jit(solution)/shard_map/ppermute | solution.py:29
  165.1 6.8 %collective-permute-start.32 = (bf16[64,512]{1,0:T(8,128)(2,1)S(1)}, bf16[64,512]{1,0:T(8,128)(2,1)S(1)}, u32[]{:S(2)}, u32[]{:S(2)}) collective-permute-start(bf16[64,512]{1,0:T(8,128)(2,1)S(1)} %get-tuple-element.13), channel_id=1, source_target_pairs={{0,16},{1,17},{2,18},{3,19},{4,20},{5,21},{6,22},{7,23},{8,24},{9,... | collective-permute-start | bytes 196616 | tf_op jit(solution)/shard_map/ppermute | solution.py:29
  168.2 4.3 %collective-permute-start.33 = (bf16[64,512]{1,0:T(8,128)(2,1)S(1)}, bf16[64,512]{1,0:T(8,128)(2,1)S(1)}, u32[]{:S(2)}, u32[]{:S(2)}) collective-permute-start(bf16[64,512]{1,0:T(8,128)(2,1)S(1)} %get-tuple-element.13), channel_id=1, source_target_pairs={{0,24},{1,25},{2,26},{3,27},{4,28},{5,29},{6,30},{7,31},{8,0},{9,1... | collective-permute-start | bytes 196616 | tf_op jit(solution)/shard_map/ppermute | solution.py:29
  173.5 2.9 %collective-permute-start.34 = (f32[64,256]{1,0:T(8,128)S(1)}, f32[64,256]{1,0:T(8,128)S(1)}, u32[]{:S(2)}, u32[]{:S(2)}) collective-permute-start(f32[64,256]{1,0:T(8,128)S(1)} %get-tuple-element.9), channel_id=1, source_target_pairs={{0,1},{1,0},{2,3},{3,2},{4,5},{5,4},{6,7},{7,6},{8,9},{9,8},{10,11... | collective-permute-start | bytes 196616 | tf_op jit(solution)/shard_map/ppermute | solution.py:29
  173.6 5.5 %collective-permute-start.35 = (f32[64,256]{1,0:T(8,128)S(1)}, f32[64,256]{1,0:T(8,128)S(1)}, u32[]{:S(2)}, u32[]{:S(2)}) collective-permute-start(f32[64,256]{1,0:T(8,128)S(1)} %get-tuple-element.30), channel_id=1, source_target_pairs={{0,4},{1,5},{2,6},{3,7},{4,0},{5,1},{6,2},{7,3},{8,12},{9,13},{10,... | collective-permute-start | bytes 196616 | tf_op jit(solution)/shard_map/ppermute | solution.py:29
  176.4 4.1 %collective-permute-start.36 = (f32[64,256]{1,0:T(8,128)S(1)}, f32[64,256]{1,0:T(8,128)S(1)}, u32[]{:S(2)}, u32[]{:S(2)}) collective-permute-start(f32[64,256]{1,0:T(8,128)S(1)} %get-tuple-element.31), channel_id=1, source_target_pairs={{0,5},{1,4},{2,7},{3,6},{4,1},{5,0},{6,3},{7,2},{8,13},{9,12},{10,... | collective-permute-start | bytes 196616 | tf_op jit(solution)/shard_map/ppermute | solution.py:29
